TPU v7x, 256 devices: a whole 4x4x8 slice. The times are simulated.
256 devices in a mesh: section: 32 (over x, z_hi, core), tp: 8 (over z_lo, y).
Axes of the slice: x: 4, y: 4, z: 8 (z_hi: 4, z_lo: 2; z = z_hi * 2 + z_lo), core: 2. Of those that a mesh axis runs over, the one named last changes fastest.
Arguments:
- carried: bfloat16 [32, 256, 5120], P('section', 'tp'), may hold values from -6 to 6
- carried_segments: int32 [32, 256], P('section'), may hold values from 0 to 31, as said below
- fresh_batch: bfloat16 [2, 256, 5120], P(None, 'tp'), may hold values from -6 to 6
- fresh_segments: int32 [2, 256], replicated, may hold values from 0 to 31, as said below
- qkv_weight: bfloat16 [32, 5120, 3, 2048], P('section', None, None, 'tp'), may hold values from -3.354102 to 3.354102
- out_weight: bfloat16 [32, 2048, 5120], P('section', 'tp'), may hold values from -0.09375 to 0.09375
- norm_gain: bfloat16 [32, 2560], P('section'), may hold values from 0.099609375 to 1.8984375
Outputs:
- layer_outputs: bfloat16 [2, 32, 256, 5120], P(None, 'section', 'tp')
- shadow_outputs: bfloat16 [32, 256, 5120], P('section', 'tp')
Inputs may be any that keep to these rules, and one draw needn't show every extreme that they name: `carried_segments`: document ids of each micro-batch's 512 tokens, read in token order across its two halves, start at 0, never fall, and rise by one at each document start; every micro-batch holds exactly 32 documents. `fresh_segments`: the same law for the entering micro-batch.
All inputs are finite; a program needn't handle non-finite values.
Results may differ from a plain program's by a relative error of at most 0.019.
Values may be sent and summed in bfloat16 or wider, within the bound.
A program may use at most 128 MiB of HBM per device.

v0:
```python
import jax
import jax.numpy as jnp
from jax import lax
from jax.sharding import PartitionSpec as P

HD = 128


eps = 1e-05
rope_base = 10000.0


def copy_for_each(array, axis):
    copies = jnp.broadcast_to(array, (lax.axis_size(axis), *array.shape))
    return lax.all_to_all(copies, axis, split_axis=0, concat_axis=0, tiled=True)


def in_order(blocks, dim):
    lengths = list(blocks.shape[1:])
    lengths[dim] *= blocks.shape[0]
    return jnp.moveaxis(blocks, 0, dim).reshape(lengths)


def gather_directly(array, axis, dim):
    blocks = copy_for_each(array, axis)
    return in_order(blocks, dim)


def from_partner(value, axis, apart):
    mask = 2**apart
    pairs = [(source, source ^ mask) for source in range(lax.axis_size(axis))]
    return lax.ppermute(value, axis, pairs)


def shifted(array, axis, by):
    count = lax.axis_size(axis)
    pairs = [(i, i + by) for i in range(count) if 0 <= i + by < count]
    return lax.ppermute(array, axis, pairs)


def normalize(values, gain):
    widened = values.astype(jnp.float32)
    power = jnp.mean(widened * widened, axis=-1, keepdims=True)
    return (widened * lax.rsqrt(power + eps) * gain.astype(jnp.float32)).astype(jnp.bfloat16)


def rotate(values, positions):
    half_dim = values.shape[-1] // 2
    frequency = rope_base ** (-(jnp.arange(half_dim, dtype=jnp.float32) * 2.0 / values.shape[-1]))
    angles = positions.astype(jnp.float32)[:, None] * frequency[None, :]
    cosine = jnp.cos(angles)[:, None, :]
    sine = jnp.sin(angles)[:, None, :]
    leading = values[..., :half_dim]
    trailing = values[..., half_dim:]
    return jnp.concatenate(
        [leading * cosine - trailing * sine, trailing * cosine + leading * sine], axis=-1
    )


def attend(projected, positions, segments):
    count = projected.shape[0]
    width = projected.shape[1] // 3
    parts = projected.reshape(count, 3, width // HD, HD)
    queries = rotate(parts[:, 0], positions).astype(jnp.bfloat16)
    keyed = rotate(parts[:, 1], positions).astype(jnp.bfloat16)
    values = parts[:, 2].astype(jnp.bfloat16)
    scores = jnp.einsum(
        "qhd,khd->hqk", queries, keyed, preferred_element_type=jnp.float32
    ) * HD ** (-0.5)
    visible = (positions[None, :] <= positions[:, None]) & (segments[None, :] == segments[:, None])
    masked = jnp.where(visible[None], scores, -1e30)
    highest = jnp.max(masked, axis=-1, keepdims=True)
    weights = jnp.where(visible[None], jnp.exp(masked - highest), 0.0)
    shares = (weights / jnp.sum(weights, axis=-1, keepdims=True)).astype(jnp.bfloat16)
    mixed = jnp.einsum("hqk,khd->qhd", shares, values, preferred_element_type=jnp.float32)
    return mixed.astype(jnp.bfloat16).reshape(count, width)


def ordered(leading, mine, other):
    return jnp.where(leading, jnp.concatenate([mine, other]), jnp.concatenate([other, mine]))


def run_layer(own_rows, own_segments, own_gain, weights_in, weights_out, parity):
    groups = lax.axis_size("tp")
    block = own_rows.shape[0]
    leading = parity == 0
    matrix = weights_in.reshape(weights_in.shape[0], -1)
    width = weights_out.shape[0]
    half_rows = gather_directly(own_rows, "tp", 0)
    other_half, other_segments, other_gain = from_partner(
        (half_rows, own_segments, own_gain), "section", 0
    )
    whole = jnp.concatenate(
        [jnp.where(leading, half_rows, other_half), jnp.where(leading, other_half, half_rows)],
        axis=0,
    )
    gain_full = ordered(leading, own_gain, other_gain)
    segments = ordered(leading, own_segments, other_segments)
    normed = normalize(whole, gain_full)
    projected = jnp.dot(normed, matrix, preferred_element_type=jnp.float32)
    total_rows = projected.shape[0]
    positions = jnp.arange(total_rows, dtype=jnp.int32)
    mixed = attend(projected, positions, segments)
    arranged = (
        mixed.reshape(2, groups, block, width).transpose(1, 0, 2, 3).reshape(total_rows, width)
    )
    summed = lax.psum_scatter(
        jnp.dot(arranged, weights_out, preferred_element_type=jnp.float32).astype(jnp.bfloat16),
        "tp",
        scatter_dimension=0,
        tiled=True,
    ).astype(jnp.float32)
    keep = jnp.where(leading, summed[:block], summed[block:])
    give = jnp.where(leading, summed[block:], summed[:block])
    taken = from_partner(give.astype(jnp.bfloat16), "section", 0).astype(give.dtype)
    return (own_rows.astype(jnp.float32) + (keep + taken)).astype(jnp.bfloat16)


def per_device(
    carried, carried_segments, fresh_batch, fresh_segments, qkv_weight, out_weight, norm_gain
):
    placed = lax.axis_index("section")
    parity = placed % 2
    section_index = placed // 2
    rows_one = carried[0]
    segments_one = carried_segments[0]
    own_gain = norm_gain[0]
    weights_in = qkv_weight[0]
    weights_out = out_weight[0]
    first_out = run_layer(rows_one, segments_one, own_gain, weights_in, weights_out, parity)
    moved_rows, moved_segments = shifted((first_out, segments_one), "section", 2)
    entering_rows = lax.dynamic_index_in_dim(fresh_batch, parity, 0, keepdims=False)
    entering_segments = lax.dynamic_index_in_dim(fresh_segments, parity, 0, keepdims=False)
    at_start = section_index == 0
    rows_two = jnp.where(at_start, entering_rows, moved_rows)
    segments_two = jnp.where(at_start, entering_segments, moved_segments)
    second_out = run_layer(rows_two, segments_two, own_gain, weights_in, weights_out, parity)
    shadow = shifted(second_out, "section", -2)
    stacked = jnp.stack([first_out, second_out])[:, None]
    return (stacked, shadow[None])


def solution(mesh):
    return jax.shard_map(
        per_device,
        mesh=mesh,
        in_specs=(
            P("section", "tp", None),
            P("section", None),
            P(None, "tp", None),
            P(),
            P("section", None, None, "tp"),
            P("section", "tp", None),
            P("section", None),
        ),
        out_specs=(P(None, "section", "tp", None), P("section", "tp", None)),
        check_vma=False,
    )
```

profile of v0, /device:TPU:1, one launch (start us, length us, event | category | flops | bytes accessed | tf_op | source)
XLA Modules:
  0.0 332.7 jit_solution(17667022592043183052)
XLA Ops:
  7.2 1.4 broadcast_in_dim.36
  8.7 37.7 %all_to_all.10 = bf16[8,32,5120]{2,1,0:T(8,128)(2,1)} all-to-all(bf16[8,32,5120]{2,1,0:T(8,128)(2,1)S(1)} %broadcast_in_dim.36), channel_id=1, replica_groups=mesh['section'=32,'tp'=8] {'tp'}, dimensions={0} | all-to-all | bytes 5242880 | tf_op jit(solution)/shard_map/all_to_all | solution.py:15
  46.4 2.4 collective-permute-start
  50.0 10.8 %copy.16 = bf16[1,5120,3,256]{1,3,2,0:T(8,128)(2,1)} copy(bf16[1,5120,3,256]{3,1,2,0:T(8,128)(2,1)} %param.11) | data formatting | bytes 15728640 | tf_op args[4]
  61.1 3.0 broadcast_select_fusion.3
  65.8 4.4 %fusion.12 = f32[512,3,2,128]{0,3,2,1:T(8,128)S(1)} fusion(bf16[3,2,128,5120]{3,2,1,0:T(8,128)(2,1)S(1)} %bitcast.68, f32[5120]{0:T(1024)S(1)} %fusion.66, f32[512]{0:T(512)S(1)} %add_rsqrt_fusion.1, bf16[256,5120]{1,0:T(8,128)(2,1)S(1)} %get-tuple-element.9, bf16[256,5120]{1,0:T(8,128)(2,1)S(1)} %get-tuple-element.8), kind=kOutput, calls=%fused_computation.17 | convolution fusion | flops 4044881920 | bytes 14702592 | tf_op jit(solution)/shard_map/dot_general | solution.py:100
  71.4 3.5 %fusion.87 = (f32[2,512]{1,0:T(2,128)S(1)}, f32[2,512,512]{1,2,0:T(8,128)}) fusion(pred[512,512]{0,1:T(8,128)(4,1)S(1)} %fusion.29, bf16[512,2,64]{0,2,1:T(8,128)(2,1)S(1)} %get-tuple-element.19, bf16[512,2,64]{0,2,1:T(8,128)(2,1)S(1)} %get-tuple-element.18, bf16[512,2,64]{0,2,1:T(8,128)(2,1)S(1)} %get-tuple-element.24, ...), kind=kOutput, calls=%fused_computation.109 | convolution fusion | flops 137888256 | bytes 2887680 | tf_op jit(solution)/shard_map/sub | solution.py:73
  74.9 2.1 fusion.22
  77.4 3.9 %convolution_convert_fusion.1 = bf16[512,5120]{1,0:T(8,128)(2,1)} fusion(bf16[512,256]{1,0:T(8,128)(2,1)S(1)} %bitcast.75, bf16[1,256,5120]{2,1,0:T(8,128)(2,1)S(1)} %copy-done), kind=kOutput, calls=%fused_computation.13 | convolution fusion | flops 1344798720 | bytes 8126464 | tf_op jit(solution)/shard_map/dot_general | solution.py:108
  81.3 65.0 %reduce-scatter.3.cloned.1.call-done = bf16[64,5120]{1,0:T(8,128)(2,1)} async-done(((bf16[512,5120]{1,0:T(8,128)(2,1)}), bf16[64,5120]{1,0:T(8,128)(2,1)}) %reduce-scatter.3.cloned.1.call-update) | async-done | bytes 655376 | tf_op jit(solution)/shard_map/reduce_scatter | solution.py:107
  148.5 1.3 collective-permute-done.3
  149.9 5.0 %collective-permute-start.4 = (bf16[32,5120]{1,0:T(8,128)(2,1)S(1)}, bf16[32,5120]{1,0:T(8,128)(2,1)}, u32[]{:S(2)}, u32[]{:S(2)}) collective-permute-start(bf16[32,5120]{1,0:T(8,128)(2,1)S(1)} %add_convert_fusion.1), channel_id=1, source_target_pairs={{0,16},{8,24},{16,32},{24,40},{32,48},{40,56},{48,64},{56,72},{64,... | collective-permute-start | bytes 983048 | tf_op jit(solution)/shard_map/ppermute | solution.py:38
  154.9 8.3 %collective-permute-done.4 = bf16[32,5120]{1,0:T(8,128)(2,1)} collective-permute-done((bf16[32,5120]{1,0:T(8,128)(2,1)S(1)}, bf16[32,5120]{1,0:T(8,128)(2,1)}, u32[]{:S(2)}, u32[]{:S(2)}) %collective-permute-start.4) | collective-permute-done | bytes 327712 | tf_op jit(solution)/shard_map/ppermute | solution.py:38
  164.5 39.3 %all_to_all.11 = bf16[8,32,5120]{2,1,0:T(8,128)(2,1)S(1)} all-to-all(bf16[8,32,5120]{2,1,0:T(8,128)(2,1)S(1)} %broadcast_in_dim.40), channel_id=1, replica_groups=mesh['section'=32,'tp'=8] {'tp'}, dimensions={0} | all-to-all | bytes 5242880 | tf_op jit(solution)/shard_map/all_to_all | solution.py:15
  203.8 2.4 collective-permute-start.5
  206.2 5.2 %collective-permute-start.6 = (s32[256]{0:T(256)S(1)}, s32[256]{0:T(256)S(1)}, u32[]{:S(2)}, u32[]{:S(2)}) collective-permute-start(s32[256]{0:T(256)S(1)} %bitcast.83), channel_id=1, source_target_pairs={{0,16},{8,24},{16,32},{24,40},{32,48},{40,56},{48,64},{56,72},{64,... | collective-permute-start | bytes 3080 | tf_op jit(solution)/shard_map/ppermute | solution.py:38
  216.8 4.4 %fusion.9 = f32[512,3,2,128]{0,3,2,1:T(8,128)S(1)} fusion(bf16[3,2,128,5120]{3,2,1,0:T(8,128)(2,1)S(1)} %bitcast.71, f32[512]{0:T(512)S(1)} %add_rsqrt_fusion, f32[5120]{0:T(1024)S(1)} %copy-done.5, bf16[256,5120]{1,0:T(8,128)(2,1)S(1)} %get-tuple-element.7, bf16[256,5120]{1,0:T(8,128)(2,1)S(1)} %get-tuple-element.6), kind=kOutput, calls=%fused_computation.15 | convolution fusion | flops 4044881920 | bytes 14702592 | tf_op jit(solution)/shard_map/dot_general | solution.py:100
  222.5 3.8 %fusion.92 = (f32[2,512]{1,0:T(2,128)S(1)}, f32[2,512,512]{1,2,0:T(8,128)}) fusion(pred[512,512]{0,1:T(8,128)(4,1)} %fusion.28, bf16[512,2,64]{0,2,1:T(8,128)(2,1)} %get-tuple-element.15, bf16[512,2,64]{0,2,1:T(8,128)(2,1)} %get-tuple-element.14, bf16[512,2,64]{0,2,1:T(8,128)(2,1)} %get-tuple-element.22, bf16[512,2,64]{0,2,1:T(8,128)(2,1)} %get-tuple-element.23), kind=kOutput, calls=%fused_computation.110 | convolution fusion | flops 137888256 | bytes 2887680 | tf_op jit(solution)/shard_map/sub | solution.py:73
  226.3 2.8 fusion.23
  232.1 3.8 %convolution_convert_fusion = bf16[512,5120]{1,0:T(8,128)(2,1)} fusion(bf16[512,256]{1,0:T(8,128)(2,1)S(1)} %bitcast.76, bf16[1,256,5120]{2,1,0:T(8,128)(2,1)S(1)} %copy-done), kind=kOutput, calls=%fused_computation.12 | convolution fusion | flops 1344798720 | bytes 8126464 | tf_op jit(solution)/shard_map/dot_general | solution.py:108
  235.9 66.4 %reduce-scatter.5.cloned.1.call-done = bf16[64,5120]{1,0:T(8,128)(2,1)} async-done(((bf16[512,5120]{1,0:T(8,128)(2,1)}), bf16[64,5120]{1,0:T(8,128)(2,1)}) %reduce-scatter.5.cloned.1.call-update) | async-done | bytes 655376 | tf_op jit(solution)/shard_map/reduce_scatter | solution.py:107
  304.4 1.3 collective-permute-done.8
  305.8 1.3 collective-permute-start.9
  308.0 17.2 %collective-permute-done.9 = bf16[32,5120]{1,0:T(8,128)(2,1)S(1)} collective-permute-done((bf16[32,5120]{1,0:T(8,128)(2,1)S(1)}, bf16[32,5120]{1,0:T(8,128)(2,1)S(1)}, u32[]{:S(2)}, u32[]{:S(2)}) %collective-permute-start.9) | collective-permute-done | bytes 327712 | tf_op jit(solution)/shard_map/ppermute | solution.py:38
  (79 shorter events, 21.7 us)
Async XLA Ops:
  7.2 70.2 %copy-start = (bf16[1,256,5120]{2,1,0:T(8,128)(2,1)S(1)}, bf16[1,256,5120]{2,1,0:T(8,128)(2,1)}, u32[]{:S(2)}) copy-start(bf16[1,256,5120]{2,1,0:T(8,128)(2,1)} %param.12) | copy-start | bytes 7864324
  7.2 139.1 %reduce-scatter.3.cloned.1.call-start = ((), (), s32[]{:S(2)}) async-start(), calls=%async_computation.4 | async-start | bytes 5898240 | tf_op jit(solution)/shard_map/reduce_scatter | solution.py:107
  8.6 40.1 %copy-start.6 = (bf16[1,2560]{1,0:T(2,128)(2,1)S(1)}, bf16[1,2560]{1,0:T(2,128)(2,1)}, u32[]{:S(2)}) copy-start(bf16[1,2560]{1,0:T(2,128)(2,1)} %param.13) | copy-start | bytes 15364
  8.7 40.3 %copy-start.7 = (s32[1,256]{1,0:T(1,128)S(1)}, s32[1,256]{1,0:T(1,128)}, u32[]{:S(2)}) copy-start(s32[1,256]{1,0:T(1,128)} %param.8) | copy-start | bytes 3076
  46.4 14.7 %collective-permute-start = (bf16[256,5120]{1,0:T(8,128)(2,1)}, bf16[256,5120]{1,0:T(8,128)(2,1)}, u32[]{:S(2)}, u32[]{:S(2)}) collective-permute-start(bf16[256,5120]{1,0:T(8,128)(2,1)} %bitcast.1), channel_id=1, source_target_pairs={{0,8},{8,0},{16,24},{24,16},{32,40},{40,32},{48,56},{56,48},{64,72... | collective-permute-start | bytes 7864328 | tf_op jit(solution)/shard_map/ppermute | solution.py:32
  48.8 12.2 %collective-permute-start.1 = (bf16[2560]{0:T(1024)(128)(2,1)S(1)}, bf16[2560]{0:T(1024)(128)(2,1)S(1)}, u32[]{:S(2)}, u32[]{:S(2)}) collective-permute-start(bf16[2560]{0:T(1024)(128)(2,1)S(1)} %reduce), channel_id=1, source_target_pairs={{0,8},{8,0},{16,24},{24,16},{32,40},{40,32},{48,56},{56,48},{64,72... | collective-permute-start | bytes 15368 | tf_op jit(solution)/shard_map/ppermute | solution.py:32
  48.9 11.9 %collective-permute-start.2 = (s32[256]{0:T(256)S(1)}, s32[256]{0:T(256)S(1)}, u32[]{:S(2)}, u32[]{:S(2)}) collective-permute-start(s32[256]{0:T(256)S(1)} %bitcast.81), channel_id=1, source_target_pairs={{0,8},{8,0},{16,24},{24,16},{32,40},{40,32},{48,56},{56,48},{64,72... | collective-permute-start | bytes 3080 | tf_op jit(solution)/shard_map/ppermute | solution.py:32
  60.8 4.4 %slice-start = ((s8[7864320]{0:T(1024)(128)(4,1)}), s8[4194304]{0:T(1024)(128)(4,1)S(1)}, s32[]{:S(2)}) async-start(s8[7864320]{0:T(1024)(128)(4,1)} %bitcast.66), calls=%async_computation.6 | async-start | bytes 8388608
  61.1 4.2 %copy-start.4 = (f32[5120]{0:T(1024)}, f32[5120]{0:T(1024)S(1)}, u32[]{:S(2)}) copy-start(f32[5120]{0:T(1024)S(1)} %fusion.66) | copy-start | bytes 61444
  61.1 4.7 %slice-start.1 = ((s8[7864320]{0:T(1024)(128)(4,1)}), s8[3670016]{0:T(1024)(128)(4,1)S(1)}, s32[]{:S(2)}) async-start(s8[7864320]{0:T(1024)(128)(4,1)} %bitcast.66), calls=%async_computation.7 | async-start | bytes 7340032
  81.3 68.5 %copy-start.1 = (bf16[1,32,5120]{2,1,0:T(8,128)(2,1)S(1)}, bf16[1,32,5120]{2,1,0:T(8,128)(2,1)}, u32[]{:S(2)}) copy-start(bf16[1,32,5120]{2,1,0:T(8,128)(2,1)} %param.7) | copy-start | bytes 983044
  81.3 221.0 %reduce-scatter.5.cloned.1.call-start = ((), (), s32[]{:S(2)}) async-start(), calls=%async_computation.5 | async-start | bytes 5898240 | tf_op jit(solution)/shard_map/reduce_scatter | solution.py:107
  147.5 2.2 collective-permute-start.3
  149.9 13.3 %collective-permute-start.4 = (bf16[32,5120]{1,0:T(8,128)(2,1)S(1)}, bf16[32,5120]{1,0:T(8,128)(2,1)}, u32[]{:S(2)}, u32[]{:S(2)}) collective-permute-start(bf16[32,5120]{1,0:T(8,128)(2,1)S(1)} %add_convert_fusion.1), channel_id=1, source_target_pairs={{0,16},{8,24},{16,32},{24,40},{32,48},{40,56},{48,64},{56,72},{64,... | collective-permute-start | bytes 983048 | tf_op jit(solution)/shard_map/ppermute | solution.py:38
  164.5 46.9 %copy-start.8 = (s32[2,256]{1,0:T(2,128)S(1)}, s32[2,256]{1,0:T(2,128)}, u32[]{:S(2)}) copy-start(s32[2,256]{1,0:T(2,128)} %param.10) | copy-start | bytes 6148
  164.5 51.9 %slice-start.2 = ((s8[7864320]{0:T(1024)(128)(4,1)}), s8[4194304]{0:T(1024)(128)(4,1)S(1)}, s32[]{:S(2)}) async-start(s8[7864320]{0:T(1024)(128)(4,1)} %bitcast.69), calls=%async_computation.8 | async-start | bytes 8388608
  203.8 11.0 %collective-permute-start.5 = (bf16[256,5120]{1,0:T(8,128)(2,1)S(1)}, bf16[256,5120]{1,0:T(8,128)(2,1)S(1)}, u32[]{:S(2)}, u32[]{:S(2)}) collective-permute-start(bf16[256,5120]{1,0:T(8,128)(2,1)S(1)} %bitcast.65), channel_id=1, source_target_pairs={{0,8},{8,0},{16,24},{24,16},{32,40},{40,32},{48,56},{56,48},{64,72... | collective-permute-start | bytes 7864328 | tf_op jit(solution)/shard_map/ppermute | solution.py:32
  206.2 5.9 %collective-permute-start.6 = (s32[256]{0:T(256)S(1)}, s32[256]{0:T(256)S(1)}, u32[]{:S(2)}, u32[]{:S(2)}) collective-permute-start(s32[256]{0:T(256)S(1)} %bitcast.83), channel_id=1, source_target_pairs={{0,16},{8,24},{16,32},{24,40},{32,48},{40,56},{48,64},{56,72},{64,... | collective-permute-start | bytes 3080 | tf_op jit(solution)/shard_map/ppermute | solution.py:38
  212.1 1.7 collective-permute-start.7
  214.7 2.0 slice-start.3
  215.3 1.5 copy-start.5
  221.2 1.3 copy-start.2
  303.6 2.1 collective-permute-start.8
  305.8 19.4 %collective-permute-start.9 = (bf16[32,5120]{1,0:T(8,128)(2,1)S(1)}, bf16[32,5120]{1,0:T(8,128)(2,1)S(1)}, u32[]{:S(2)}, u32[]{:S(2)}) collective-permute-start(bf16[32,5120]{1,0:T(8,128)(2,1)S(1)} %add_convert_fusion), channel_id=1, source_target_pairs={{16,0},{24,8},{32,16},{40,24},{48,32},{56,40},{64,48},{72,56},{80,... | collective-permute-start | bytes 983048 | tf_op jit(solution)/shard_map/ppermute | solution.py:38
  (1 other events, 1.2 us)
Sparse Core Ops, SparseCore 0:
  81.4 64.8 reduce-scatter.2
  236.0 66.2 reduce-scatter.4
where the time goes:
time: 333 us
  waiting for transfers between devices  161 us (48%)
  blocking collectives  77 us (23%)
  matrix products  28.7 us (9%)
  starting transfers between devices  19.6 us (6%)
  local copies, waits for them, and re-layouts  17.7 us (5%)
  other arithmetic  14.4 us (4%)
  between operations  14.4 us (4%)
    reduce_scatter x2, waiting for transfers between devices, run_layer(): lax.psum_scatter(jnp.dot(arranged, weights_out, preferred_element_type=jn...  131 us
    all_to_all x2, blocking collectives, copy_for_each(): return lax.all_to_all(copies, axis, split_axis=0, concat_axis=0, tiled=True)  77 us
    ppermute x3, waiting for transfers between devices, shifted(): return lax.ppermute(array, axis, pairs)  26.2 us
    unnamed x28, local copies, waits for them, and re-layouts  12.6 us
    ppermute x3, starting transfers between devices, shifted(): return lax.ppermute(array, axis, pairs)  11.5 us
    dot_general x2, matrix products, run_layer(): projected = jnp.dot(normed, matrix, preferred_element_type=jnp.float32)  8.78 us
    ppermute x7, starting transfers between devices, from_partner(): return lax.ppermute(value, axis, pairs)  8.08 us
    dot_general x2, matrix products, run_layer(): jnp.dot(arranged, weights_out, preferred_element_type=jnp.float32)  7.74 us
  transfers between devices with their start and end apart: 12, of which 8 were waited for; matrix products, arithmetic and copies ran while one was open for 4% of the time, Pallas kernels for 0%

commit v1 on v0

v1 whole, which is shorter than its diff:
```python
import jax
import jax.numpy as jnp
import numpy as np
from jax import lax
from jax.experimental import pallas as pl
from jax.experimental.pallas import tpu as pltpu
from jax.sharding import PartitionSpec as P

HD = 128
EPS = 1e-05
ROPE_BASE = 10000.0
MASKED = -1e30
MESH = pl.DeviceIdType.MESH
CHUNKS = 4
CHUNK_GAP = 5.5
STEP_GAP = 4.0


def rope_tables(tokens):
    frequency = np.float32(ROPE_BASE) ** (-(np.arange(HD // 2, dtype=np.float32) * np.float32(2.0) / np.float32(HD)))
    angles = np.arange(tokens, dtype=np.float32)[:, None] * frequency.astype(np.float32)[None, :]
    cosine = np.cos(angles.astype(np.float64)).astype(np.float32)
    sine = np.sin(angles.astype(np.float64)).astype(np.float32)
    cosines = np.concatenate([cosine, cosine], axis=1)
    sines = np.concatenate([-sine, sine], axis=1)
    return np.stack([cosines, sines], axis=0)


def make_kernel(n_sections, width, block, heads_each):
    C = CHUNKS
    half = 8 * block
    cw = width // C
    gw = width // 2
    cols = heads_each * HD

    def kernel(
        carried, own_segments, fresh, fresh_segments, w_hbm, o_hbm, gain, tables,
        out, shadow,
        X, W, O, ACC, SS, XG, PB, RSA, RSB, RSZ, YS, SH, KV, KVO, MX, S, BIAS, G, SEGS, TAB,
        local_sem, send_sem, recv_sem,
    ):
        p = lax.axis_index("section")
        t = lax.axis_index("tp")
        core = lax.rem(p, 2)
        s = lax.div(p, 2)
        zl = lax.div(t, 4)
        y = lax.rem(t, 4)
        first = s == 0
        last = s == n_sections - 1

        def at(z, yy):
            return z * 4 + lax.rem(yy, 4)

        other_z = 1 - zl
        own, rz = t, at(other_z, y)
        up, down, far = at(zl, y + 1), at(zl, y + 3), at(zl, y + 2)
        z_up, z_down, z_far = at(other_z, y + 1), at(other_z, y + 3), at(other_z, y + 2)
        dev_z, dev_up, dev_down = (p, rz), (p, up), (p, down)
        partner = (p + 1 - 2 * core, t)
        ahead = (lax.rem(p + 2, 2 * n_sections), t)
        behind = (lax.rem(p + 2 * n_sections - 2, 2 * n_sections), t)

        def rows(b):
            return pl.ds(pl.multiple_of(b * block, block), block)

        def span(c):
            return pl.ds(c * cw, cw)

        counts = {"local": 0, "remote": 0}
        unsent = []

        def local_copy(src, dst):
            n = counts["local"]
            counts["local"] += 1
            return pltpu.make_async_copy(src, dst, local_sem.at[n])

        def message(src, dst, device):
            n = counts["remote"]
            counts["remote"] += 1
            copy = pltpu.make_async_remote_copy(
                src_ref=src, dst_ref=dst, send_sem=send_sem.at[n], recv_sem=recv_sem.at[n],
                device_id=device, device_id_type=MESH,
            )
            return copy

        def send(copy):
            copy.start()
            unsent.append(copy)

        own_rows = []
        for c in range(C):
            copy = local_copy(carried.at[0, :, span(c)], X.at[0, c, rows(own)])
            copy.start()
            own_rows.append(copy)
        w_own = []
        for c in range(C):
            copy = local_copy(w_hbm.at[:, span(c)], W.at[core, :, span(c)])
            copy.start()
            w_own.append(copy)
        o_own = local_copy(o_hbm.at[0], O.at[core])
        o_own.start()
        table_copy = local_copy(tables.at[:, pl.ds(pl.multiple_of(core * half, half), half)], TAB)
        table_copy.start()
        fresh_rows = [local_copy(fresh.at[core, :, span(c)], X.at[1, c, rows(own)]) for c in range(C)]

        @pl.when(first)
        def _():
            for copy in fresh_rows:
                copy.start()

        G[core] = jnp.broadcast_to(gain[...].astype(jnp.float32), (8, gw))
        SEGS[0, core] = jnp.broadcast_to(own_segments[...], (8, half))

        barrier = pltpu.get_barrier_semaphore()
        for device in (dev_z, dev_up, dev_down, partner, ahead, behind):
            pl.semaphore_signal(barrier, inc=1, device_id=device, device_id_type=MESH)
        pl.semaphore_wait(barrier, 6)

        ag = {}
        for l in range(2):
            for c in range(C):
                def block_of(b, device, l=l, c=c):
                    ref = X.at[l, c, rows(b)]
                    return message(ref, ref, device)
                ag[l, c] = dict(
                    z=block_of(own, dev_z),
                    down=block_of(own, dev_up),
                    up=block_of(own, dev_down),
                    z_down=block_of(rz, dev_up),
                    z_up=block_of(rz, dev_down),
                    far=block_of(down, dev_up) if c % 2 == 0 else block_of(up, dev_down),
                    z_far=block_of(far, dev_z),
                )

        def spread(l, c):
            for name in ("z", "down", "up"):
                send(ag[l, c][name])

        def relay(l, c):
            ag[l, c]["z"].wait_recv()
            send(ag[l, c]["z_down"])
            send(ag[l, c]["z_up"])
            ag[l, c]["down"].wait_recv()
            if c % 2 == 0:
                send(ag[l, c]["far"])
            ag[l, c]["up"].wait_recv()
            if c % 2 == 1:
                send(ag[l, c]["far"])

        def relay_far(l, c):
            ag[l, c]["far"].wait_recv()
            send(ag[l, c]["z_far"])

        def gathered(l, c):
            for name in ("z_down", "z_up", "z_far"):
                ag[l, c][name].wait_recv()

        for c in range(C):
            own_rows[c].wait()
            spread(0, c)
        w_other = []
        for c in range(C):
            copy = message(w_hbm.at[:, span(c)], W.at[core, :, span(c)], partner)
            send(copy)
            w_other.append(copy)
            if c == 0:
                gain_other = message(G.at[core], G.at[core], partner)
                send(gain_other)
                segments_other = message(SEGS.at[0, core], SEGS.at[0, core], partner)
                send(segments_other)
        o_other = message(o_hbm.at[0], O.at[core], partner)
        send(o_other)
        segments_ahead = message(SEGS.at[0], SEGS.at[1], ahead)

        def multiply(l, c):
            g0 = (c * cw) // gw
            scale = G[g0, 0:1, (c * cw) % gw:(c * cw) % gw + cw]

            def body(i, _):
                r = pl.ds(pl.multiple_of(i * 32, 32), 32)
                x = X[l, c, r].astype(jnp.float32)
                XG[r] = (x * scale).astype(jnp.bfloat16)
                square = x * x
                total = square[:, 0:HD]
                for k in range(1, cw // HD):
                    total = total + square[:, k * HD:(k + 1) * HD]
                if c == 0:
                    SS[r] = total
                else:
                    SS[r] = SS[r] + total
                return 0

            lax.fori_loop(0, half // 32, body, 0)
            for g in range(2):
                for j in range(3):
                    part = jnp.dot(XG[...], W[g, j, c * cw:(c + 1) * cw], preferred_element_type=jnp.float32)
                    if c == 0:
                        ACC[g, j] = part
                    else:
                        ACC[g, j] = ACC[g, j] + part

        def attend(l):
            power = jnp.sum(SS[...], axis=-1, keepdims=True) * (1.0 / width)
            factor = lax.rsqrt(power + EPS)
            heads = [(g, i) for g in range(2) for i in range(heads_each)]

            def rotated(v):
                return v * TAB[0] + pltpu.roll(v, HD // 2, 1) * TAB[1]

            for h, (g, i) in enumerate(heads):
                KV[l, 1, h] = (ACC[g, 2, :, i * HD:(i + 1) * HD] * factor).astype(jnp.bfloat16)
            values = message(KV.at[l, 1], KVO.at[l, 1], partner)
            send(values)
            for h, (g, i) in enumerate(heads):
                KV[l, 0, h] = rotated(ACC[g, 1, :, i * HD:(i + 1) * HD] * factor).astype(jnp.bfloat16)
            keys = message(KV.at[l, 0], KVO.at[l, 0], partner)
            send(keys)
            mine = jnp.broadcast_to(SEGS[l, core, 0:1], (HD, half)).astype(jnp.float32).T[:, 0:1]
            row_of = lax.broadcasted_iota(jnp.int32, (half, half), 0)
            column_of = lax.broadcasted_iota(jnp.int32, (half, half), 1)
            same = mine == SEGS[l, core, 0:1].astype(jnp.float32)
            BIAS[0] = jnp.where(same & (column_of <= row_of), 0.0, MASKED)
            elder = SEGS[l, 1 - core, 0:1].astype(jnp.float32)
            elder = jnp.where(core == 1, elder, -1.0)
            BIAS[1] = jnp.where(mine == elder, 0.0, MASKED)
            for h, (g, i) in enumerate(heads):
                q = rotated(ACC[g, 0, :, i * HD:(i + 1) * HD] * factor).astype(jnp.bfloat16)
                MX[:, h * HD:(h + 1) * HD] = q
                scores = lax.dot_general(q, KV[l, 0, h], (((1,), (1,)), ((), ())), preferred_element_type=jnp.float32)
                S[h] = scores * HD ** (-0.5) + BIAS[0]
            values.wait_recv()
            keys.wait_recv()
            for h in range(len(heads)):
                q = MX[:, h * HD:(h + 1) * HD]
                near = S[h]
                away = lax.dot_general(q, KVO[l, 0, h], (((1,), (1,)), ((), ())), preferred_element_type=jnp.float32)
                away = away * HD ** (-0.5) + BIAS[1]
                top = jnp.maximum(jnp.max(near, axis=-1, keepdims=True), jnp.max(away, axis=-1, keepdims=True))
                near = jnp.exp(near - top)
                away = jnp.exp(away - top)
                total = jnp.sum(near, axis=-1, keepdims=True) + jnp.sum(away, axis=-1, keepdims=True)
                mixed = jnp.dot(near.astype(jnp.bfloat16), KV[l, 1, h], preferred_element_type=jnp.float32)
                mixed = mixed + jnp.dot(away.astype(jnp.bfloat16), KVO[l, 1, h], preferred_element_type=jnp.float32)
                MX[:, h * HD:(h + 1) * HD] = (mixed / total).astype(jnp.bfloat16)

        rs = {}
        for l in range(2):
            for c in range(C):
                def part(b, ref, device, l=l, c=c):
                    return message(PB.at[l, c, rows(b)], ref, device)
                even = c % 2 == 0
                rs[l, c] = dict(
                    a0=part(far if even else z_far, RSA.at[l, c, 0], dev_up),
                    a1=part(z_far if even else far, RSA.at[l, c, 1], dev_down),
                    b0=part(up, RSB.at[l, c, 0], dev_up),
                    b1=part(down, RSB.at[l, c, 1], dev_down),
                    b2=part(z_up, RSB.at[l, c, 2], dev_up),
                    b3=part(z_down, RSB.at[l, c, 3], dev_down),
                    z=part(rz, RSZ.at[l, c], dev_z),
                )
        shifts = {}
        for c in range(C):
            shifts[0, c] = message(YS.at[0, c], X.at[1, c, rows(own)], ahead)
            shifts[1, c] = message(YS.at[1, c], SH.at[c], behind)

        def f32(v):
            return v.astype(jnp.float32)

        def project(l, c):
            PB[l, c] = jnp.dot(
                MX[...], O[:, :, c * cw:(c + 1) * cw].reshape(2 * cols, cw), preferred_element_type=jnp.float32
            ).astype(jnp.bfloat16)
            m = rs[l, c]
            for name in ("a0", "a1", "b2", "b1") if c % 2 == 0 else ("a0", "a1", "b0", "b3"):
                send(m[name])

        def fold_far(l, c):
            m = rs[l, c]
            m["a0"].wait_recv()
            m["a1"].wait_recv()
            even = c % 2 == 0
            for slot, b in ((0, up if even else z_up), (1, z_down if even else down)):
                r = rows(b)
                PB[l, c, r] = (f32(PB[l, c, r]) + f32(RSA[l, c, slot])).astype(jnp.bfloat16)
            for name in ("b3", "b0") if even else ("b2", "b1"):
                send(m[name])

        def fold_z(l, c):
            m = rs[l, c]
            m["b2"].wait_recv()
            m["b3"].wait_recv()
            r = rows(rz)
            PB[l, c, r] = (f32(PB[l, c, r]) + f32(RSB[l, c, 2]) + f32(RSB[l, c, 3])).astype(jnp.bfloat16)
            send(m["z"])

        def finish(l, c):
            m = rs[l, c]
            m["b0"].wait_recv()
            m["b1"].wait_recv()
            m["z"].wait_recv()
            r = rows(own)
            total = f32(PB[l, c, r]) + f32(RSB[l, c, 0]) + f32(RSB[l, c, 1]) + f32(RSZ[l, c])
            result = (f32(X[l, c, r]) + total).astype(jnp.bfloat16)
            YS[l, c] = result
            out[l, 0, :, c * cw:(c + 1) * cw] = result

            @pl.when(jnp.logical_not(last) if l == 0 else jnp.logical_not(first))
            def _():
                shifts[l, c].start()

        def enter(c):
            @pl.when(first)
            def _():
                fresh_rows[c].wait()

            @pl.when(jnp.logical_not(first))
            def _():
                shifts[0, c].wait_recv()

            spread(1, c)

        def leave(c):
            @pl.when(jnp.logical_not(last))
            def _():
                shifts[1, c].wait_recv()
                shadow[0, :, c * cw:(c + 1) * cw] = SH[c]

            @pl.when(last)
            def _():
                shadow[0, :, c * cw:(c + 1) * cw] = jnp.zeros((block, cw), jnp.bfloat16)

        def run(steps):
            order = sorted((c * CHUNK_GAP + k * STEP_GAP, c, k) for c in range(C) for k in range(len(steps)))
            for _, c, k in order:
                steps[k](c)

        for c in range(C):
            relay(0, c)
        gain_other.wait_recv()

        def compute_first(c):
            gathered(0, c)
            w_own[c].wait()
            w_other[c].wait_recv()
            multiply(0, c)

        for c in range(C):
            relay_far(0, c)
            if c >= 1:
                compute_first(c - 1)
        compute_first(C - 1)
        segments_other.wait_recv()

        @pl.when(jnp.logical_not(last))
        def _():
            segments_ahead.start()

        table_copy.wait()
        attend(0)
        o_own.wait()
        o_other.wait_recv()

        def compute_second(c):
            gathered(1, c)
            multiply(1, c)

        run([
            lambda c: project(0, c),
            lambda c: fold_far(0, c),
            lambda c: fold_z(0, c),
            lambda c: finish(0, c),
            enter,
            lambda c: relay(1, c),
            lambda c: relay_far(1, c),
            compute_second,
        ])

        @pl.when(first)
        def _():
            for b in range(2):
                SEGS[1, b] = jnp.broadcast_to(fresh_segments[b:b + 1], (8, half))

        @pl.when(jnp.logical_not(first))
        def _():
            segments_ahead.wait_recv()

        attend(1)
        run([
            lambda c: project(1, c),
            lambda c: fold_far(1, c),
            lambda c: fold_z(1, c),
            lambda c: finish(1, c),
            leave,
        ])
        for copy in unsent:
            copy.wait_send()

        @pl.when(jnp.logical_not(last))
        def _():
            segments_ahead.wait_send()
            for c in range(C):
                shifts[0, c].wait_send()

        @pl.when(jnp.logical_not(first))
        def _():
            for c in range(C):
                shifts[1, c].wait_send()

    bf, f4 = jnp.bfloat16, jnp.float32
    heads = 2 * heads_each
    scratch = [
        pltpu.VMEM((2, C, half, cw), bf),
        pltpu.VMEM((2, 3, width, cols), bf),
        pltpu.VMEM((2, cols, width), bf),
        pltpu.VMEM((2, 3, half, cols), f4),
        pltpu.VMEM((half, HD), f4),
        pltpu.VMEM((half, cw), bf),
        pltpu.VMEM((2, C, half, cw), bf),
        pltpu.VMEM((2, C, 2, block, cw), bf),
        pltpu.VMEM((2, C, 4, block, cw), bf),
        pltpu.VMEM((2, C, block, cw), bf),
        pltpu.VMEM((2, C, block, cw), bf),
        pltpu.VMEM((C, block, cw), bf),
        pltpu.VMEM((2, 2, heads, half, HD), bf),
        pltpu.VMEM((2, 2, heads, half, HD), bf),
        pltpu.VMEM((half, heads * HD), bf),
        pltpu.VMEM((heads, half, half), f4),
        pltpu.VMEM((2, half, half), f4),
        pltpu.VMEM((2, 8, gw), f4),
        pltpu.VMEM((2, 2, 8, half), jnp.int32),
        pltpu.VMEM((2, half, HD), f4),
        pltpu.SemaphoreType.DMA((3 * C + 2,)),
        pltpu.SemaphoreType.DMA((2 * (7 + 7 + 1) * C + 2 * 2 + C + 4,)),
        pltpu.SemaphoreType.DMA((2 * (7 + 7 + 1) * C + 2 * 2 + C + 4,)),
    ]
    return kernel, scratch


def per_device(carried, carried_segments, fresh_batch, fresh_segments, qkv_weight, out_weight, norm_gain):
    _, block, width = carried.shape
    cols = qkv_weight.shape[-1]
    n_sections = lax.axis_size("section") // 2
    kernel, scratch = make_kernel(n_sections, width, block, cols // HD)
    weights = jnp.transpose(qkv_weight[0], (1, 0, 2))
    tables = jnp.asarray(rope_tables(16 * block))
    vmem = pl.BlockSpec(memory_space=pltpu.VMEM)
    hbm = pl.BlockSpec(memory_space=pl.ANY)
    out, shadow = pl.pallas_call(
        kernel,
        name="relay",
        out_shape=(
            jax.ShapeDtypeStruct((2, 1, block, width), jnp.bfloat16),
            jax.ShapeDtypeStruct((1, block, width), jnp.bfloat16),
        ),
        in_specs=[hbm, vmem, hbm, vmem, hbm, hbm, vmem, hbm],
        out_specs=(vmem, vmem),
        scratch_shapes=scratch,
        compiler_params=pltpu.CompilerParams(
            collective_id=0, has_side_effects=True, vmem_limit_bytes=60 * 2**20
        ),
    )(carried, carried_segments, fresh_batch, fresh_segments, weights, out_weight, norm_gain, tables)
    return out, shadow


def solution(mesh):
    return jax.shard_map(
        per_device,
        mesh=mesh,
        in_specs=(
            P("section", "tp", None),
            P("section", None),
            P(None, "tp", None),
            P(),
            P("section", None, None, "tp"),
            P("section", "tp", None),
            P("section", None),
        ),
        out_specs=(P(None, "section", "tp", None), P("section", "tp", None)),
        check_vma=False,
    )
```

time: 333 us -> 142 us (0.43)
  waiting for transfers between devices: 161 us -> 0 us
  Pallas kernels: 0 us -> 138 us
  blocking collectives: 77 us -> 0 us
  matrix products: 28.7 us -> 0 us
  starting transfers between devices: 19.6 us -> 0 us
  other arithmetic: 14.4 us -> 0 us
  local copies, waits for them, and re-layouts: 17.7 us -> 3.68 us
  between operations: 14.4 us -> 0.64 us
    pallas_call x0 -> x1, Pallas kernels: none -> 138 us  [per_device(): pl.pallas_call(kernel, name='relay', out_shape=(jax.ShapeDtypeStruct((2,...]
    reduce_scatter x2 -> x0, waiting for transfers between devices: 131 us -> none  [run_layer(): lax.psum_scatter(jnp.dot(arranged, weights_out, preferred_element_type=jn...]
    all_to_all x2 -> x0, blocking collectives: 77 us -> none  [copy_for_each(): return lax.all_to_all(copies, axis, split_axis=0, concat_axis=0, tiled=True)]
    ppermute x10 -> x0, waiting for transfers between devices: 29.5 us -> none  [the longest x3 26.2 us: shifted(): return lax.ppermute(array, axis, pairs)]
    dot_general x6 -> x0, matrix products: 21.4 us -> none  [the longest x2 8.78 us: run_layer(): projected = jnp.dot(normed, matrix, preferred_element_type=jnp.float32)]
    ppermute x10 -> x0, starting transfers between devices: 19.5 us -> none  [the longest x3 11.5 us: shifted(): return lax.ppermute(array, axis, pairs)]
    unnamed x28 -> x2, local copies, waits for them, and re-layouts: 12.6 us -> 3.68 us
    sub x2 -> x0, matrix products: 7.33 us -> none  [attend(): weights = jnp.where(visible[None], jnp.exp(masked - highest), 0.0)]
  transfers between devices with their start and end apart: 12 -> 0, of which waited for: 8 -> 0; matrix products, arithmetic and copies ran while one was open for 4% -> 0% of each run, Pallas kernels for 0% -> 0%
where the time goes in v1:
time: 142 us
  Pallas kernels  138 us (97%)
  local copies, waits for them, and re-layouts  3.68 us (3%)
    pallas_call x1, Pallas kernels, per_device(): pl.pallas_call(kernel, name='relay', out_shape=(jax.ShapeDtypeStruct((2,...  138 us
    unnamed x2, local copies, waits for them, and re-layouts  3.68 us

profile of v1, /device:TPU:1, one launch (start us, length us, event | category | flops | bytes accessed | tf_op | source)
XLA Modules:
  0.0 142.1 jit_solution(15492875346753475278)
XLA Ops:
  0.6 137.8 %relay.1 = (bf16[2,1,32,5120]{3,2,1,0:T(8,128)(2,1)}, bf16[1,32,5120]{2,1,0:T(8,128)(2,1)}) custom-call(bf16[1,32,5120]{2,1,0:T(8,128)(2,1)} %carried.1, s32[1,256]{1,0:T(1,128)} %own_segments.1, bf16[2,32,5120]{2,1,0:T(8,128)(2,1)} %fresh.1, s32[2,256]{1,0:T(2,128)} %fresh_segments.1, bf16[3,5120,256]{2,1,0:T(8,128)(2,1)} %bitcast.3, ...), custom_call_target="tpu_custom_call" | custom-call | tf_op jit(solution)/shard_map/relay/pallas_call | solution.py:448
  138.5 2.0 %copy.12 = bf16[2,1,32,5120]{3,2,1,0:T(8,128)(2,1)} copy(bf16[2,1,32,5120]{3,2,1,0:T(8,128)(2,1)} %get-tuple-element.4) | data formatting | bytes 1310720
  140.4 1.7 %copy.13 = bf16[1,32,5120]{2,1,0:T(8,128)(2,1)} copy(bf16[1,32,5120]{2,1,0:T(8,128)(2,1)} %get-tuple-element.5) | data formatting | bytes 655360

commit v2 on v1

v2 whole, which is shorter than its diff:
```python
import jax
import jax.numpy as jnp
import numpy as np
from jax import lax
from jax.experimental import pallas as pl
from jax.experimental.pallas import tpu as pltpu
from jax.sharding import PartitionSpec as P

HD = 128
EPS = 1e-05
ROPE_BASE = 10000.0
MASKED = -1e30
MESH = pl.DeviceIdType.MESH
CHUNKS = 10
FIRST_ORDER = (
    (4, 6), (4, 5), (4, 2), (4, 0), (4, 4), (4, 8), (4, 7), (4, 9), (6, 6), (5, 6),
    (6, 4), (4, 1), (6, 8), (4, 3), (6, 7), (6, 0), (6, 9), (7, 6), (6, 5), (5, 9),
    (7, 4), (6, 2), (6, 1), (7, 7), (6, 3), (5, 4), (5, 8), (5, 7), (7, 9), (7, 8),
    (7, 0), (5, 5), (8, 6), (7, 5), (7, 2), (5, 2), (7, 3), (8, 9), (5, 3), (7, 1),
    (5, 0), (5, 1), (8, 4), (8, 8), (8, 7), (8, 5), (8, 2), (8, 3), (8, 0), (8, 1),
)
MIDDLE_ORDER = (
    (0, 2), (0, 1), (0, 0), (1, 2), (1, 1), (1, 0), (0, 3), (0, 4), (2, 2), (2, 1),
    (0, 6), (2, 0), (1, 3), (3, 2), (1, 4), (0, 8), (3, 1), (3, 0), (1, 6), (2, 3),
    (0, 5), (4, 2), (0, 7), (2, 4), (4, 1), (2, 6), (3, 3), (1, 8), (3, 4), (1, 5),
    (1, 7), (0, 9), (4, 0), (2, 8), (2, 5), (6, 2), (3, 6), (2, 7), (1, 9), (4, 3),
    (5, 1), (5, 0), (3, 5), (2, 9), (3, 7), (4, 6), (6, 3), (3, 8), (4, 4), (6, 0),
    (3, 9), (6, 1), (7, 2), (4, 5), (5, 6), (7, 1), (4, 7), (6, 5), (5, 2), (4, 8),
    (7, 3), (6, 4), (6, 6), (5, 3), (4, 9), (6, 7), (6, 8), (5, 5), (7, 5), (5, 4),
    (7, 0), (7, 4), (8, 2), (6, 9), (7, 6), (5, 8), (5, 7), (8, 3), (5, 9), (7, 8),
    (7, 7), (8, 1), (8, 5), (7, 9), (8, 0), (8, 4), (8, 6), (8, 8), (8, 7), (8, 9),
)
LAST_ORDER = (
    (0, 1), (0, 4), (0, 0), (1, 1), (1, 4), (0, 7), (1, 0), (2, 1), (0, 3), (0, 2),
    (2, 4), (2, 0), (3, 1), (1, 7), (0, 6), (3, 4), (1, 3), (1, 2), (2, 7), (3, 0),
    (0, 8), (1, 6), (2, 3), (0, 5), (2, 2), (3, 7), (4, 1), (0, 9), (4, 4), (2, 6),
    (3, 3), (1, 8), (1, 5), (3, 2), (1, 9), (2, 8), (4, 7), (2, 5), (3, 6), (2, 9),
    (4, 0), (4, 3), (3, 8), (3, 5), (4, 6), (4, 2), (3, 9), (4, 8), (4, 5), (4, 9),
)


def rope_tables(tokens):
    frequency = np.float32(ROPE_BASE) ** (-(np.arange(HD // 2, dtype=np.float32) * np.float32(2.0) / np.float32(HD)))
    angles = np.arange(tokens, dtype=np.float32)[:, None] * frequency.astype(np.float32)[None, :]
    cosine = np.cos(angles.astype(np.float64)).astype(np.float32)
    sine = np.sin(angles.astype(np.float64)).astype(np.float32)
    cosines = np.concatenate([cosine, cosine], axis=1)
    sines = np.concatenate([-sine, sine], axis=1)
    return np.stack([cosines, sines], axis=0)


def make_kernel(n_sections, width, block, heads_each):
    C = CHUNKS
    half = 8 * block
    cw = width // C
    gw = width // 2
    cols = heads_each * HD

    def kernel(
        carried, own_segments, fresh, fresh_segments, w_hbm, o_hbm, gain, tables,
        out, shadow,
        X, W, O, ACC, SS, XG, PB, R, YS, SH, KV, KVO, MX, S, BIAS, G, SEGS, TAB,
        local_sem, send_sem, recv_sem,
    ):
        p = lax.axis_index("section")
        t = lax.axis_index("tp")
        core = lax.rem(p, 2)
        s = lax.div(p, 2)
        zl = lax.div(t, 4)
        y = lax.rem(t, 4)
        first = s == 0
        last = s == n_sections - 1

        def at(z, yy):
            return z * 4 + lax.rem(yy, 4)

        other_z = 1 - zl
        own, rz = t, at(other_z, y)
        up, down, far = at(zl, y + 1), at(zl, y + 3), at(zl, y + 2)
        z_up, z_down, z_far = at(other_z, y + 1), at(other_z, y + 3), at(other_z, y + 2)
        dev_z, dev_up, dev_down = (p, rz), (p, up), (p, down)
        partner = (p + 1 - 2 * core, t)
        ahead = (lax.rem(p + 2, 2 * n_sections), t)
        behind = (lax.rem(p + 2 * n_sections - 2, 2 * n_sections), t)

        def rows(b):
            return pl.ds(pl.multiple_of(b * block, block), block)

        def span(c):
            return pl.ds(c * cw, cw)

        counts = {"local": 0, "sent": 0, "received": 0}

        def fresh_sem(kind, sems):
            n = counts[kind]
            counts[kind] += 1
            return sems.at[n]

        def local_copy(src, dst):
            return pltpu.make_async_copy(src, dst, fresh_sem("local", local_sem))

        unsent_early = []

        def send_group():
            return fresh_sem("sent", send_sem)

        def arrival():
            return fresh_sem("received", recv_sem)

        def message(src, dst, device, sent, arrived):
            return pltpu.make_async_remote_copy(
                src_ref=src, dst_ref=dst, send_sem=sent, recv_sem=arrived,
                device_id=device, device_id_type=MESH,
            )

        def wait_for(ref, sem):
            pltpu.make_async_copy(ref, ref, sem).wait()

        own_rows = []
        for c in range(C):
            copy = local_copy(carried.at[0, :, span(c)], X.at[0, c, rows(own)])
            copy.start()
            own_rows.append(copy)
        w_own = local_copy(w_hbm, W.at[core])
        w_own.start()
        o_own = local_copy(o_hbm.at[0], O.at[core])
        o_own.start()
        table_copy = local_copy(tables.at[:, pl.ds(pl.multiple_of(core * half, half), half)], TAB)
        table_copy.start()
        fresh_sem_all = fresh_sem("local", local_sem)
        fresh_rows = [
            pltpu.make_async_copy(fresh.at[core, :, span(c)], X.at[1, c, rows(own)], fresh_sem_all) for c in range(C)
        ]

        @pl.when(first)
        def _():
            for copy in fresh_rows:
                copy.start()

        G[core] = jnp.broadcast_to(gain[...].astype(jnp.float32), (8, gw))
        SEGS[0, core] = jnp.broadcast_to(own_segments[...], (8, half))

        barrier = pltpu.get_barrier_semaphore()
        for device in (dev_z, dev_up, dev_down, partner, ahead, behind):
            pl.semaphore_signal(barrier, inc=1, device_id=device, device_id_type=MESH)
        with jax.named_scope("entry"):
            pl.semaphore_wait(barrier, 6)

        ag_sent = [send_group() for _ in range(2)]
        rs_sent = [send_group() for _ in range(2)]
        shift_sent = [send_group() for _ in range(2)]
        ag_sem = {(c, k): arrival() for c in range(C) for k in ("z", "y", "far", "rest")}
        rs_sem = {(c, k): arrival() for c in range(C) for k in ("far", "z", "own")}

        ag = {}
        for l in range(2):
            for c in range(C):
                def block_of(b, device, kind, l=l, c=c):
                    ref = X.at[l, c, rows(b)]
                    return message(ref, ref, device, ag_sent[l], ag_sem[c, kind])
                even = c % 2 == 0
                ag[l, c] = dict(
                    z=block_of(own, dev_z, "z"),
                    down=block_of(own, dev_up, "y" if even else "rest"),
                    up=block_of(own, dev_down, "rest" if even else "y"),
                    z_down=block_of(rz, dev_up, "rest"),
                    z_up=block_of(rz, dev_down, "rest"),
                    far=block_of(down, dev_up, "far") if even else block_of(up, dev_down, "far"),
                    z_far=block_of(far, dev_z, "rest"),
                )

        def spread(l, c):
            for name in ("z", "down", "up"):
                ag[l, c][name].start()

        def relay_z(l, c):
            wait_for(X.at[l, c, rows(rz)], ag_sem[c, "z"])
            ag[l, c]["z_down"].start()
            ag[l, c]["z_up"].start()

        def relay_y(l, c):
            wait_for(X.at[l, c, rows(down if c % 2 == 0 else up)], ag_sem[c, "y"])
            ag[l, c]["far"].start()

        def relay_far(l, c):
            wait_for(X.at[l, c, rows(far)], ag_sem[c, "far"])
            ag[l, c]["z_far"].start()

        def gathered(l, c):
            wait_for(X.at[l, c, pl.ds(0, 4 * block)], ag_sem[c, "rest"])

        def spread_first(c):
            own_rows[c].wait()
            spread(0, c)

        w_sent = send_group()
        w_sem = [arrival() for _ in range(C)]
        small_sent, small_sem = [send_group() for _ in range(4)], [arrival() for _ in range(4)]
        w_other = {}
        for c in (c for k, c in FIRST_ORDER if k == 8):
            w_other[c] = message(w_hbm.at[:, span(c)], W.at[core, :, span(c)], partner, w_sent, w_sem[c])
            w_other[c].start()
            if len(w_other) == 1:
                gain_other = message(G.at[core], G.at[core], partner, small_sent[0], small_sem[0])
                gain_other.start()
                segments_other = message(
                    SEGS.at[0, core], SEGS.at[0, core], partner, small_sent[1], small_sem[1]
                )
                segments_other.start()
        o_other = message(o_hbm.at[0], O.at[core], partner, small_sent[2], small_sem[2])
        o_other.start()
        segments_ahead = message(SEGS.at[0], SEGS.at[1], ahead, small_sent[3], small_sem[3])

        begun = set()

        def multiply(l, c):
            opening = l not in begun
            begun.add(l)
            g0 = (c * cw) // gw
            scale = G[g0, 0:1, (c * cw) % gw:(c * cw) % gw + cw]

            def body(i, _):
                r = pl.ds(pl.multiple_of(i * 32, 32), 32)
                x = X[l, c, r].astype(jnp.float32)
                XG[r] = (x * scale).astype(jnp.bfloat16)
                square = x * x
                total = square[:, 0:HD]
                for k in range(1, cw // HD):
                    total = total + square[:, k * HD:(k + 1) * HD]
                if opening:
                    SS[r] = total
                else:
                    SS[r] = SS[r] + total
                return 0

            lax.fori_loop(0, half // 32, body, 0)
            for g in range(2):
                for j in range(3):
                    part = jnp.dot(XG[...], W[g, j, c * cw:(c + 1) * cw], preferred_element_type=jnp.float32)
                    if opening:
                        ACC[g, j] = part
                    else:
                        ACC[g, j] = ACC[g, j] + part

        def attend(l):
            power = jnp.sum(SS[...], axis=-1, keepdims=True) * (1.0 / width)
            factor = lax.rsqrt(power + EPS)
            heads = [(g, i) for g in range(2) for i in range(heads_each)]

            def rotated(v):
                return v * TAB[0] + pltpu.roll(v, HD // 2, 1) * TAB[1]

            for h, (g, i) in enumerate(heads):
                KV[l, 1, h] = (ACC[g, 2, :, i * HD:(i + 1) * HD] * factor).astype(jnp.bfloat16)
            values = message(KV.at[l, 1], KVO.at[l, 1], partner, send_group(), arrival())
            keys = message(KV.at[l, 0], KVO.at[l, 0], partner, send_group(), arrival())

            @pl.when(core == 0)
            def _():
                values.start()

            for h, (g, i) in enumerate(heads):
                KV[l, 0, h] = rotated(ACC[g, 1, :, i * HD:(i + 1) * HD] * factor).astype(jnp.bfloat16)

            @pl.when(core == 0)
            def _():
                keys.start()

            unsent_early.append(values)
            unsent_early.append(keys)
            mine = jnp.broadcast_to(SEGS[l, core, 0:1], (HD, half)).astype(jnp.float32).T[:, 0:1]
            row_of = lax.broadcasted_iota(jnp.int32, (half, half), 0)
            column_of = lax.broadcasted_iota(jnp.int32, (half, half), 1)
            same = mine == SEGS[l, core, 0:1].astype(jnp.float32)
            BIAS[0] = jnp.where(same & (column_of <= row_of), 0.0, MASKED)

            @pl.when(core == 1)
            def _():
                BIAS[1] = jnp.where(mine == SEGS[l, 0, 0:1].astype(jnp.float32), 0.0, MASKED)

            for h, (g, i) in enumerate(heads):
                q = rotated(ACC[g, 0, :, i * HD:(i + 1) * HD] * factor).astype(jnp.bfloat16)
                MX[:, h * HD:(h + 1) * HD] = q
                scores = lax.dot_general(q, KV[l, 0, h], (((1,), (1,)), ((), ())), preferred_element_type=jnp.float32)
                S[h] = scores * HD ** (-0.5) + BIAS[0]

            def columns(h):
                return slice(h * HD, (h + 1) * HD)

            @pl.when(core == 0)
            def _():
                for h in range(len(heads)):
                    near = S[h]
                    near = jnp.exp(near - jnp.max(near, axis=-1, keepdims=True))
                    total = jnp.sum(near, axis=-1, keepdims=True)
                    mixed = jnp.dot(near.astype(jnp.bfloat16), KV[l, 1, h], preferred_element_type=jnp.float32)
                    MX[:, columns(h)] = (mixed / total).astype(jnp.bfloat16)

            @pl.when(core == 1)
            def _():
                with jax.named_scope("keys_wait"):
                    values.wait_recv()
                    keys.wait_recv()
                for h in range(len(heads)):
                    q = MX[:, columns(h)]
                    near = S[h]
                    away = lax.dot_general(
                        q, KVO[l, 0, h], (((1,), (1,)), ((), ())), preferred_element_type=jnp.float32
                    )
                    away = away * HD ** (-0.5) + BIAS[1]
                    top = jnp.maximum(jnp.max(near, axis=-1, keepdims=True), jnp.max(away, axis=-1, keepdims=True))
                    near = jnp.exp(near - top)
                    away = jnp.exp(away - top)
                    total = jnp.sum(near, axis=-1, keepdims=True) + jnp.sum(away, axis=-1, keepdims=True)
                    mixed = jnp.dot(near.astype(jnp.bfloat16), KV[l, 1, h], preferred_element_type=jnp.float32)
                    mixed = mixed + jnp.dot(away.astype(jnp.bfloat16), KVO[l, 1, h], preferred_element_type=jnp.float32)
                    MX[:, columns(h)] = (mixed / total).astype(jnp.bfloat16)

        rs = {}
        for l in range(2):
            for c in range(C):
                def part(b, slot, device, kind, l=l, c=c):
                    return message(PB.at[l, c, rows(b)], R.at[l, c, slot], device, rs_sent[l], rs_sem[c, kind])
                even = c % 2 == 0
                rs[l, c] = dict(
                    a0=part(far if even else z_far, 0, dev_up, "far"),
                    a1=part(z_far if even else far, 1, dev_down, "far"),
                    b2=part(z_up, 2, dev_up, "z"),
                    b3=part(z_down, 3, dev_down, "z"),
                    b0=part(up, 4, dev_up, "own"),
                    b1=part(down, 5, dev_down, "own"),
                    z=part(rz, 6, dev_z, "own"),
                )
        shift_sem = [[arrival() for _ in range(C)] for _ in range(2)]
        shifts = {}
        for c in range(C):
            shifts[0, c] = message(YS.at[0, c], X.at[1, c, rows(own)], ahead, shift_sent[0], shift_sem[0][c])
            shifts[1, c] = message(YS.at[1, c], SH.at[c], behind, shift_sent[1], shift_sem[1][c])

        def f32(v):
            return v.astype(jnp.float32)

        def project(l, c):
            PB[l, c] = jnp.dot(
                MX[...], O[:, :, c * cw:(c + 1) * cw].reshape(2 * cols, cw), preferred_element_type=jnp.float32
            ).astype(jnp.bfloat16)
            m = rs[l, c]
            for name in ("a0", "a1", "b2", "b1") if c % 2 == 0 else ("a0", "a1", "b0", "b3"):
                m[name].start()

        def fold_far(l, c):
            m = rs[l, c]
            wait_for(R.at[l, c, pl.ds(0, 2)], rs_sem[c, "far"])
            even = c % 2 == 0
            for slot, b in ((0, up if even else z_up), (1, z_down if even else down)):
                r = rows(b)
                PB[l, c, r] = (f32(PB[l, c, r]) + f32(R[l, c, slot])).astype(jnp.bfloat16)
            for name in ("b3", "b0") if even else ("b2", "b1"):
                m[name].start()

        def fold_z(l, c):
            m = rs[l, c]
            wait_for(R.at[l, c, pl.ds(2, 2)], rs_sem[c, "z"])
            r = rows(rz)
            PB[l, c, r] = (f32(PB[l, c, r]) + f32(R[l, c, 2]) + f32(R[l, c, 3])).astype(jnp.bfloat16)
            m["z"].start()

        def finish(l, c):
            wait_for(R.at[l, c, pl.ds(4, 3)], rs_sem[c, "own"])
            r = rows(own)
            total = f32(PB[l, c, r]) + f32(R[l, c, 4]) + f32(R[l, c, 5]) + f32(R[l, c, 6])
            result = (f32(X[l, c, r]) + total).astype(jnp.bfloat16)
            YS[l, c] = result
            out[l, 0, :, c * cw:(c + 1) * cw] = result

            @pl.when(jnp.logical_not(last) if l == 0 else jnp.logical_not(first))
            def _():
                shifts[l, c].start()

        entered = []

        def enter(c):
            @pl.when(first)
            def _():
                if not entered:
                    wait_for(YS.at[0], fresh_sem_all)

            @pl.when(jnp.logical_not(first))
            def _():
                shifts[0, c].wait_recv()

            entered.append(c)
            spread(1, c)

        def leave(c):
            @pl.when(jnp.logical_not(last))
            def _():
                shifts[1, c].wait_recv()
                shadow[0, :, c * cw:(c + 1) * cw] = SH[c]

            @pl.when(last)
            def _():
                shadow[0, :, c * cw:(c + 1) * cw] = jnp.zeros((block, cw), jnp.bfloat16)

        def run(steps, order):
            for k, c in order:
                with jax.named_scope(f"step{k}c{c}"):
                    steps[k](c)

        gain_waited = []

        def compute_first(c):
            gathered(0, c)
            if not gain_waited:
                gain_other.wait_recv()
                gain_waited.append(True)
                w_own.wait()
            w_other[c].wait_recv()
            multiply(0, c)

        run({
            4: spread_first,
            5: lambda c: relay_z(0, c),
            6: lambda c: relay_y(0, c),
            7: lambda c: relay_far(0, c),
            8: compute_first,
        }, FIRST_ORDER)
        segments_other.wait_recv()

        @pl.when(jnp.logical_not(last))
        def _():
            segments_ahead.start()

        table_copy.wait()
        with jax.named_scope("attend_first"):
            attend(0)
        o_own.wait()
        o_other.wait_recv()

        def compute_second(c):
            gathered(1, c)
            multiply(1, c)

        run({
            0: lambda c: project(0, c),
            1: lambda c: fold_far(0, c),
            2: lambda c: fold_z(0, c),
            3: lambda c: finish(0, c),
            4: enter,
            5: lambda c: relay_z(1, c),
            6: lambda c: relay_y(1, c),
            7: lambda c: relay_far(1, c),
            8: compute_second,
        }, MIDDLE_ORDER)

        @pl.when(first)
        def _():
            for b in range(2):
                SEGS[1, b] = jnp.broadcast_to(fresh_segments[b:b + 1], (8, half))

        @pl.when(jnp.logical_not(first))
        def _():
            segments_ahead.wait_recv()

        with jax.named_scope("attend_second"):
            attend(1)
        run({
            0: lambda c: project(1, c),
            1: lambda c: fold_far(1, c),
            2: lambda c: fold_z(1, c),
            3: lambda c: finish(1, c),
            4: leave,
        }, LAST_ORDER)
        with jax.named_scope("drain"):
            for l in range(2):
                wait_for(R.at[l], ag_sent[l])
                wait_for(R.at[l], rs_sent[l])
            wait_for(W.at[core], w_sent)
            for copy in (gain_other, segments_other, o_other):
                copy.wait_send()

        @pl.when(core == 0)
        def _():
            for copy in unsent_early:
                copy.wait_send()

        @pl.when(jnp.logical_not(last))
        def _():
            segments_ahead.wait_send()
            wait_for(YS.at[0], shift_sent[0])

        @pl.when(jnp.logical_not(first))
        def _():
            wait_for(YS.at[1], shift_sent[1])

    bf, f4 = jnp.bfloat16, jnp.float32
    heads = 2 * heads_each
    scratch = [
        pltpu.VMEM((2, C, half, cw), bf),
        pltpu.VMEM((2, 3, width, cols), bf),
        pltpu.VMEM((2, cols, width), bf),
        pltpu.VMEM((2, 3, half, cols), f4),
        pltpu.VMEM((half, HD), f4),
        pltpu.VMEM((half, cw), bf),
        pltpu.VMEM((2, C, half, cw), bf),
        pltpu.VMEM((2, C, 7, block, cw), bf),
        pltpu.VMEM((2, C, block, cw), bf),
        pltpu.VMEM((C, block, cw), bf),
        pltpu.VMEM((2, 2, heads, half, HD), bf),
        pltpu.VMEM((2, 2, heads, half, HD), bf),
        pltpu.VMEM((half, heads * HD), bf),
        pltpu.VMEM((heads, half, half), f4),
        pltpu.VMEM((2, half, half), f4),
        pltpu.VMEM((2, 8, gw), f4),
        pltpu.VMEM((2, 2, 8, half), jnp.int32),
        pltpu.VMEM((2, half, HD), f4),
        pltpu.SemaphoreType.DMA((C + 4,)),
        pltpu.SemaphoreType.DMA((6 + 1 + 4 + 4,)),
        pltpu.SemaphoreType.DMA(((4 + 3 + 2 + 1) * C + 4 + 4,)),
    ]
    return kernel, scratch


def per_device(carried, carried_segments, fresh_batch, fresh_segments, qkv_weight, out_weight, norm_gain):
    _, block, width = carried.shape
    cols = qkv_weight.shape[-1]
    n_sections = lax.axis_size("section") // 2
    kernel, scratch = make_kernel(n_sections, width, block, cols // HD)
    weights = jnp.transpose(qkv_weight[0], (1, 0, 2))
    tables = jnp.asarray(rope_tables(16 * block))
    vmem = pl.BlockSpec(memory_space=pltpu.VMEM)
    hbm = pl.BlockSpec(memory_space=pltpu.HBM)
    out, shadow = pl.pallas_call(
        kernel,
        name="relay",
        out_shape=(
            jax.ShapeDtypeStruct((2, 1, block, width), jnp.bfloat16),
            jax.ShapeDtypeStruct((1, block, width), jnp.bfloat16),
        ),
        in_specs=[hbm, vmem, hbm, vmem, hbm, hbm, vmem, hbm],
        out_specs=(vmem, vmem),
        scratch_shapes=scratch,
        compiler_params=pltpu.CompilerParams(
            collective_id=0, has_side_effects=True, vmem_limit_bytes=60 * 2**20
        ),
    )(carried, carried_segments, fresh_batch, fresh_segments, weights, out_weight, norm_gain, tables)
    return out, shadow


def solution(mesh):
    return jax.shard_map(
        per_device,
        mesh=mesh,
        in_specs=(
            P("section", "tp", None),
            P("section", None),
            P(None, "tp", None),
            P(),
            P("section", None, None, "tp"),
            P("section", "tp", None),
            P("section", None),
        ),
        out_specs=(P(None, "section", "tp", None), P("section", "tp", None)),
        check_vma=False,
    )
```

time: 142 us -> 125 us (0.88)
  Pallas kernels: 138 us -> 120 us
    pallas_call x1, Pallas kernels: 138 us -> 120 us  [per_device(): pl.pallas_call(kernel, name='relay', out_shape=(jax.ShapeDtypeStruct((2,...]
where the time goes in v2:
time: 125 us; the launch traced here: 124 us
  Pallas kernels  120 us (96%)
  local copies, waits for them, and re-layouts  3.68 us (3%)
    pallas_call x1, Pallas kernels, per_device(): pl.pallas_call(kernel, name='relay', out_shape=(jax.ShapeDtypeStruct((2,...  120 us
    unnamed x2, local copies, waits for them, and re-layouts  3.68 us

profile of v2, /device:TPU:1, one launch (start us, length us, event | category | flops | bytes accessed | tf_op | source)
XLA Modules:
  0.0 124.3 jit_solution(16682098401992631247)
XLA Ops:
  0.6 120.0 %relay.1 = (bf16[2,1,32,5120]{3,2,1,0:T(8,128)(2,1)}, bf16[1,32,5120]{2,1,0:T(8,128)(2,1)}) custom-call(bf16[1,32,5120]{2,1,0:T(8,128)(2,1)} %carried.1, s32[1,256]{1,0:T(1,128)} %own_segments.1, bf16[2,32,5120]{2,1,0:T(8,128)(2,1)} %fresh.1, s32[2,256]{1,0:T(2,128)} %fresh_segments.1, bf16[3,5120,256]{2,1,0:T(8,128)(2,1)} %bitcast.3, ...), custom_call_target="tpu_custom_call" | custom-call | tf_op jit(solution)/shard_map/relay/pallas_call | solution.py:533
  120.6 2.0 %copy.12 = bf16[2,1,32,5120]{3,2,1,0:T(8,128)(2,1)} copy(bf16[2,1,32,5120]{3,2,1,0:T(8,128)(2,1)} %get-tuple-element.4) | data formatting | bytes 1310720
  122.6 1.7 %copy.13 = bf16[1,32,5120]{2,1,0:T(8,128)(2,1)} copy(bf16[1,32,5120]{2,1,0:T(8,128)(2,1)} %get-tuple-element.5) | data formatting | bytes 655360

commit v3 on v2

--- a/solution.py
+++ b/solution.py
@@ -13,29 +13,31 @@
 MESH = pl.DeviceIdType.MESH
 CHUNKS = 10
 FIRST_ORDER = (
-    (4, 6), (4, 5), (4, 2), (4, 0), (4, 4), (4, 8), (4, 7), (4, 9), (6, 6), (5, 6),
-    (6, 4), (4, 1), (6, 8), (4, 3), (6, 7), (6, 0), (6, 9), (7, 6), (6, 5), (5, 9),
-    (7, 4), (6, 2), (6, 1), (7, 7), (6, 3), (5, 4), (5, 8), (5, 7), (7, 9), (7, 8),
-    (7, 0), (5, 5), (8, 6), (7, 5), (7, 2), (5, 2), (7, 3), (8, 9), (5, 3), (7, 1),
-    (5, 0), (5, 1), (8, 4), (8, 8), (8, 7), (8, 5), (8, 2), (8, 3), (8, 0), (8, 1),
+    (4, 6), (4, 1), (4, 7), (4, 9), (4, 4), (4, 5), (6, 1), (4, 8), (4, 3), (6, 7),
+    (4, 2), (6, 9), (4, 0), (6, 6), (5, 5), (6, 4), (6, 8), (7, 1), (6, 0), (6, 2),
+    (5, 6), (6, 5), (6, 3), (7, 7), (5, 4), (5, 9), (7, 6), (7, 9), (5, 7), (7, 4),
+    (5, 0), (7, 8), (7, 5), (5, 8), (7, 0), (5, 1), (5, 3), (8, 6), (7, 2), (8, 4),
+    (7, 3), (5, 2), (8, 9), (8, 7), (8, 5), (8, 0), (8, 8), (8, 1), (8, 3), (8, 2),
 )
 MIDDLE_ORDER = (
-    (0, 2), (0, 1), (0, 0), (1, 2), (1, 1), (1, 0), (0, 3), (0, 4), (2, 2), (2, 1),
-    (0, 6), (2, 0), (1, 3), (3, 2), (1, 4), (0, 8), (3, 1), (3, 0), (1, 6), (2, 3),
-    (0, 5), (4, 2), (0, 7), (2, 4), (4, 1), (2, 6), (3, 3), (1, 8), (3, 4), (1, 5),
-    (1, 7), (0, 9), (4, 0), (2, 8), (2, 5), (6, 2), (3, 6), (2, 7), (1, 9), (4, 3),
-    (5, 1), (5, 0), (3, 5), (2, 9), (3, 7), (4, 6), (6, 3), (3, 8), (4, 4), (6, 0),
-    (3, 9), (6, 1), (7, 2), (4, 5), (5, 6), (7, 1), (4, 7), (6, 5), (5, 2), (4, 8),
-    (7, 3), (6, 4), (6, 6), (5, 3), (4, 9), (6, 7), (6, 8), (5, 5), (7, 5), (5, 4),
-    (7, 0), (7, 4), (8, 2), (6, 9), (7, 6), (5, 8), (5, 7), (8, 3), (5, 9), (7, 8),
-    (7, 7), (8, 1), (8, 5), (7, 9), (8, 0), (8, 4), (8, 6), (8, 8), (8, 7), (8, 9),
+    (0, 9), (0, 0), (0, 5), (0, 3), (1, 9), (0, 2), (1, 0), (9, 0), (1, 5), (1, 3),
+    (9, 9), (0, 7), (9, 5), (9, 3), (0, 8), (2, 9), (1, 2), (2, 0), (2, 5), (2, 3),
+    (0, 6), (3, 9), (0, 1), (0, 4), (3, 0), (3, 3), (1, 7), (1, 8), (9, 8), (3, 5),
+    (1, 6), (2, 2), (9, 2), (4, 0), (1, 4), (1, 1), (9, 1), (2, 8), (9, 4), (4, 3),
+    (9, 6), (2, 7), (4, 5), (3, 2), (2, 4), (5, 3), (2, 1), (5, 5), (2, 6), (9, 7),
+    (6, 0), (3, 8), (4, 2), (3, 4), (6, 5), (6, 3), (3, 6), (3, 1), (3, 7), (4, 8),
+    (4, 9), (5, 2), (4, 4), (6, 2), (4, 6), (6, 8), (7, 0), (5, 0), (6, 9), (7, 3),
+    (4, 1), (6, 4), (7, 2), (4, 7), (7, 8), (6, 6), (5, 4), (7, 5), (5, 9), (6, 1),
+    (6, 7), (7, 9), (5, 8), (8, 3), (7, 4), (5, 1), (7, 6), (8, 2), (5, 6), (8, 0),
+    (7, 1), (7, 7), (5, 7), (8, 5), (8, 8), (8, 9), (8, 4), (8, 6), (8, 1), (8, 7),
 )
 LAST_ORDER = (
-    (0, 1), (0, 4), (0, 0), (1, 1), (1, 4), (0, 7), (1, 0), (2, 1), (0, 3), (0, 2),
-    (2, 4), (2, 0), (3, 1), (1, 7), (0, 6), (3, 4), (1, 3), (1, 2), (2, 7), (3, 0),
-    (0, 8), (1, 6), (2, 3), (0, 5), (2, 2), (3, 7), (4, 1), (0, 9), (4, 4), (2, 6),
-    (3, 3), (1, 8), (1, 5), (3, 2), (1, 9), (2, 8), (4, 7), (2, 5), (3, 6), (2, 9),
-    (4, 0), (4, 3), (3, 8), (3, 5), (4, 6), (4, 2), (3, 9), (4, 8), (4, 5), (4, 9),
+    (0, 5), (0, 6), (0, 9), (0, 0), (1, 5), (0, 3), (1, 9), (1, 6), (0, 2), (1, 0),
+    (9, 5), (2, 5), (9, 6), (1, 3), (2, 6), (9, 3), (0, 1), (2, 9), (1, 2), (9, 0),
+    (2, 0), (3, 5), (0, 4), (2, 3), (0, 7), (3, 6), (1, 1), (9, 2), (0, 8), (2, 2),
+    (3, 0), (3, 3), (1, 4), (9, 9), (1, 7), (4, 5), (9, 4), (2, 1), (3, 2), (1, 8),
+    (2, 4), (9, 1), (9, 7), (3, 9), (9, 8), (2, 7), (2, 8), (3, 1), (3, 4), (4, 6),
+    (3, 8), (4, 3), (3, 7), (4, 9), (4, 2), (4, 8), (4, 1), (4, 0), (4, 4), (4, 7),
 )
 
 
@@ -59,8 +61,8 @@
     def kernel(
         carried, own_segments, fresh, fresh_segments, w_hbm, o_hbm, gain, tables,
         out, shadow,
-        X, W, O, ACC, SS, XG, PB, R, YS, SH, KV, KVO, MX, S, BIAS, G, SEGS, TAB,
-        local_sem, send_sem, recv_sem,
+        X, W, O, ACC, SS, XG, PB, R, YS, SH, KV, KVO, MX, S, BIAS, G, SEGS, TAB, GIN, SIN, FIN,
+        local_sem, send_sem, recv_sem, out_sem,
     ):
         p = lax.axis_index("section")
         t = lax.axis_index("tp")
@@ -116,6 +118,9 @@
         def wait_for(ref, sem):
             pltpu.make_async_copy(ref, ref, sem).wait()
 
+        small_loads = [local_copy(gain, GIN), local_copy(own_segments, SIN), local_copy(fresh_segments, FIN)]
+        for copy in small_loads:
+            copy.start()
         own_rows = []
         for c in range(C):
             copy = local_copy(carried.at[0, :, span(c)], X.at[0, c, rows(own)])
@@ -132,19 +137,24 @@
             pltpu.make_async_copy(fresh.at[core, :, span(c)], X.at[1, c, rows(own)], fresh_sem_all) for c in range(C)
         ]
 
+        @pl.when(last)
+        def _():
+            SH[...] = jnp.zeros(SH.shape, SH.dtype)
+
         @pl.when(first)
         def _():
             for copy in fresh_rows:
                 copy.start()
-
-        G[core] = jnp.broadcast_to(gain[...].astype(jnp.float32), (8, gw))
-        SEGS[0, core] = jnp.broadcast_to(own_segments[...], (8, half))
 
         barrier = pltpu.get_barrier_semaphore()
         for device in (dev_z, dev_up, dev_down, partner, ahead, behind):
             pl.semaphore_signal(barrier, inc=1, device_id=device, device_id_type=MESH)
         with jax.named_scope("entry"):
             pl.semaphore_wait(barrier, 6)
+        for copy in small_loads:
+            copy.wait()
+        G[core] = jnp.broadcast_to(GIN[...].astype(jnp.float32), (8, gw))
+        SEGS[0, core] = jnp.broadcast_to(SIN[...], (8, half))
 
         ag_sent = [send_group() for _ in range(2)]
         rs_sent = [send_group() for _ in range(2)]
@@ -345,7 +355,7 @@
                 MX[...], O[:, :, c * cw:(c + 1) * cw].reshape(2 * cols, cw), preferred_element_type=jnp.float32
             ).astype(jnp.bfloat16)
             m = rs[l, c]
-            for name in ("a0", "a1", "b2", "b1") if c % 2 == 0 else ("a0", "a1", "b0", "b3"):
+            for name in ("a0", "a1", "b2") if c % 2 == 0 else ("a0", "a1", "b3"):
                 m[name].start()
 
         def fold_far(l, c):
@@ -355,8 +365,11 @@
             for slot, b in ((0, up if even else z_up), (1, z_down if even else down)):
                 r = rows(b)
                 PB[l, c, r] = (f32(PB[l, c, r]) + f32(R[l, c, slot])).astype(jnp.bfloat16)
-            for name in ("b3", "b0") if even else ("b2", "b1"):
-                m[name].start()
+            m["b3" if even else "b2"].start()
+
+        def give(l, c):
+            for name in ("b0", "b1"):
+                rs[l, c][name].start()
 
         def fold_z(l, c):
             m = rs[l, c]
@@ -371,7 +384,7 @@
             total = f32(PB[l, c, r]) + f32(R[l, c, 4]) + f32(R[l, c, 5]) + f32(R[l, c, 6])
             result = (f32(X[l, c, r]) + total).astype(jnp.bfloat16)
             YS[l, c] = result
-            out[l, 0, :, c * cw:(c + 1) * cw] = result
+            pltpu.make_async_copy(YS.at[l, c], out.at[l, 0, :, span(c)], out_sem.at[l]).start()
 
             @pl.when(jnp.logical_not(last) if l == 0 else jnp.logical_not(first))
             def _():
@@ -396,11 +409,8 @@
             @pl.when(jnp.logical_not(last))
             def _():
                 shifts[1, c].wait_recv()
-                shadow[0, :, c * cw:(c + 1) * cw] = SH[c]
-
-            @pl.when(last)
-            def _():
-                shadow[0, :, c * cw:(c + 1) * cw] = jnp.zeros((block, cw), jnp.bfloat16)
+
+            pltpu.make_async_copy(SH.at[c], shadow.at[0, :, span(c)], out_sem.at[2]).start()
 
         def run(steps, order):
             for k, c in order:
@@ -451,12 +461,13 @@
             6: lambda c: relay_y(1, c),
             7: lambda c: relay_far(1, c),
             8: compute_second,
+            9: lambda c: give(0, c),
         }, MIDDLE_ORDER)
 
         @pl.when(first)
         def _():
             for b in range(2):
-                SEGS[1, b] = jnp.broadcast_to(fresh_segments[b:b + 1], (8, half))
+                SEGS[1, b] = jnp.broadcast_to(FIN[b:b + 1], (8, half))
 
         @pl.when(jnp.logical_not(first))
         def _():
@@ -470,12 +481,15 @@
             2: lambda c: fold_z(1, c),
             3: lambda c: finish(1, c),
             4: leave,
+            9: lambda c: give(1, c),
         }, LAST_ORDER)
         with jax.named_scope("drain"):
             for l in range(2):
                 wait_for(R.at[l], ag_sent[l])
                 wait_for(R.at[l], rs_sent[l])
             wait_for(W.at[core], w_sent)
+            for ref, n in ((YS.at[0], 0), (YS.at[1], 1), (SH, 2)):
+                wait_for(ref, out_sem.at[n])
             for copy in (gain_other, segments_other, o_other):
                 copy.wait_send()
 
@@ -514,11 +528,42 @@
         pltpu.VMEM((2, 8, gw), f4),
         pltpu.VMEM((2, 2, 8, half), jnp.int32),
         pltpu.VMEM((2, half, HD), f4),
-        pltpu.SemaphoreType.DMA((C + 4,)),
+        pltpu.VMEM((1, gw), bf),
+        pltpu.VMEM((1, half), jnp.int32),
+        pltpu.VMEM((2, half), jnp.int32),
+        pltpu.SemaphoreType.DMA((C + 7,)),
         pltpu.SemaphoreType.DMA((6 + 1 + 4 + 4,)),
         pltpu.SemaphoreType.DMA(((4 + 3 + 2 + 1) * C + 4 + 4,)),
+        pltpu.SemaphoreType.DMA((3,)),
     ]
     return kernel, scratch
+
+
+def store(count):
+    def kernel(*refs):
+        sources, results, held, sem = refs[:count], refs[count:2 * count], refs[2 * count:3 * count], refs[-1]
+        for i in range(count):
+            pltpu.make_async_copy(sources[i], held[i], sem.at[0, i]).start()
+        for i in range(count):
+            pltpu.make_async_copy(sources[i], held[i], sem.at[0, i]).wait()
+            pltpu.make_async_copy(held[i], results[i], sem.at[1, i]).start()
+        for i in range(count):
+            pltpu.make_async_copy(held[i], results[i], sem.at[1, i]).wait()
+
+    return kernel
+
+
+def carry_over(arrays):
+    hbm = pl.BlockSpec(memory_space=pl.ANY)
+    return pl.pallas_call(
+        store(len(arrays)),
+        name="store",
+        out_shape=tuple(jax.ShapeDtypeStruct(a.shape, a.dtype) for a in arrays),
+        in_specs=[hbm] * len(arrays),
+        out_specs=(hbm,) * len(arrays),
+        scratch_shapes=[pltpu.VMEM(a.shape, a.dtype) for a in arrays] + [pltpu.SemaphoreType.DMA((2, len(arrays)))],
+        compiler_params=pltpu.CompilerParams(vmem_limit_bytes=60 * 2**20),
+    )(*arrays)
 
 
 def per_device(carried, carried_segments, fresh_batch, fresh_segments, qkv_weight, out_weight, norm_gain):
@@ -528,7 +573,6 @@
     kernel, scratch = make_kernel(n_sections, width, block, cols // HD)
     weights = jnp.transpose(qkv_weight[0], (1, 0, 2))
     tables = jnp.asarray(rope_tables(16 * block))
-    vmem = pl.BlockSpec(memory_space=pltpu.VMEM)
     hbm = pl.BlockSpec(memory_space=pltpu.HBM)
     out, shadow = pl.pallas_call(
         kernel,
@@ -537,14 +581,14 @@
             jax.ShapeDtypeStruct((2, 1, block, width), jnp.bfloat16),
             jax.ShapeDtypeStruct((1, block, width), jnp.bfloat16),
         ),
-        in_specs=[hbm, vmem, hbm, vmem, hbm, hbm, vmem, hbm],
-        out_specs=(vmem, vmem),
+        in_specs=[hbm] * 8,
+        out_specs=(hbm, hbm),
         scratch_shapes=scratch,
         compiler_params=pltpu.CompilerParams(
             collective_id=0, has_side_effects=True, vmem_limit_bytes=60 * 2**20
         ),
     )(carried, carried_segments, fresh_batch, fresh_segments, weights, out_weight, norm_gain, tables)
-    return out, shadow
+    return carry_over((out, shadow))
 
 
 def solution(mesh):

time: 125 us -> 120 us (0.960)
  local copies, waits for them, and re-layouts: 3.68 us -> 0 us
    unnamed x2 -> x0, local copies, waits for them, and re-layouts: 3.68 us -> none
    pallas_call x1, Pallas kernels: 120 us -> 117 us  [per_device(): pl.pallas_call(kernel, name='relay', out_shape=(jax.ShapeDtypeStruct((2,...]
    pallas_call x0 -> x1, Pallas kernels: none -> 2.06 us  [carry_over(): pl.pallas_call(store(len(arrays)), name='store', out_shape=tuple((jax.Sha...]
where the time goes in v3:
time: 120 us
  Pallas kernels  119 us (99%)
    pallas_call x1, Pallas kernels, per_device(): pl.pallas_call(kernel, name='relay', out_shape=(jax.ShapeDtypeStruct((2,...  117 us

profile of v3, /device:TPU:1, one launch (start us, length us, event | category | flops | bytes accessed | tf_op | source)
XLA Modules:
  0.0 119.9 jit_solution(8320943443619006053)
XLA Ops:
  0.6 117.0 %relay.1 = (bf16[2,1,32,5120]{3,2,1,0:T(8,128)(2,1)}, bf16[1,32,5120]{2,1,0:T(8,128)(2,1)}) custom-call(bf16[1,32,5120]{2,1,0:T(8,128)(2,1)} %carried.1, s32[1,256]{1,0:T(1,128)} %own_segments.1, bf16[2,32,5120]{2,1,0:T(8,128)(2,1)} %fresh.1, s32[2,256]{1,0:T(2,128)} %fresh_segments.1, bf16[3,5120,256]{2,1,0:T(8,128)(2,1)} %bitcast.3, ...), custom_call_target="tpu_custom_call" | custom-call | tf_op jit(solution)/shard_map/relay/pallas_call | solution.py:577
  117.6 2.1 %store.1 = (bf16[2,1,32,5120]{3,2,1,0:T(8,128)(2,1)}, bf16[1,32,5120]{2,1,0:T(8,128)(2,1)}) custom-call(bf16[2,1,32,5120]{3,2,1,0:T(8,128)(2,1)} %get-tuple-element.4.refs_0_, bf16[1,32,5120]{2,1,0:T(8,128)(2,1)} %get-tuple-element.5.refs_1_), custom_call_target="tpu_custom_call" | custom-call | tf_op jit(solution)/shard_map/store/pallas_call | solution.py:558

commit v4 on v3

--- a/solution.py
+++ b/solution.py
@@ -20,25 +20,28 @@
     (7, 3), (5, 2), (8, 9), (8, 7), (8, 5), (8, 0), (8, 8), (8, 1), (8, 3), (8, 2),
 )
 MIDDLE_ORDER = (
-    (0, 9), (0, 0), (0, 5), (0, 3), (1, 9), (0, 2), (1, 0), (9, 0), (1, 5), (1, 3),
-    (9, 9), (0, 7), (9, 5), (9, 3), (0, 8), (2, 9), (1, 2), (2, 0), (2, 5), (2, 3),
-    (0, 6), (3, 9), (0, 1), (0, 4), (3, 0), (3, 3), (1, 7), (1, 8), (9, 8), (3, 5),
-    (1, 6), (2, 2), (9, 2), (4, 0), (1, 4), (1, 1), (9, 1), (2, 8), (9, 4), (4, 3),
-    (9, 6), (2, 7), (4, 5), (3, 2), (2, 4), (5, 3), (2, 1), (5, 5), (2, 6), (9, 7),
-    (6, 0), (3, 8), (4, 2), (3, 4), (6, 5), (6, 3), (3, 6), (3, 1), (3, 7), (4, 8),
-    (4, 9), (5, 2), (4, 4), (6, 2), (4, 6), (6, 8), (7, 0), (5, 0), (6, 9), (7, 3),
-    (4, 1), (6, 4), (7, 2), (4, 7), (7, 8), (6, 6), (5, 4), (7, 5), (5, 9), (6, 1),
-    (6, 7), (7, 9), (5, 8), (8, 3), (7, 4), (5, 1), (7, 6), (8, 2), (5, 6), (8, 0),
-    (7, 1), (7, 7), (5, 7), (8, 5), (8, 8), (8, 9), (8, 4), (8, 6), (8, 1), (8, 7),
+    (0, 5), (0, 7), (0, 6), (0, 4), (0, 3), (0, 9), (10, 5), (0, 8), (0, 2), (2, 6),
+    (2, 4), (2, 5), (0, 1), (1, 9), (0, 0), (2, 7), (10, 2), (2, 3), (1, 5), (10, 3),
+    (9, 5), (10, 4), (1, 8), (2, 2), (2, 9), (9, 9), (2, 0), (10, 0), (2, 1), (10, 1),
+    (1, 3), (10, 6), (1, 2), (9, 2), (3, 5), (2, 8), (3, 9), (9, 8), (10, 7), (3, 2),
+    (1, 6), (9, 3), (1, 4), (1, 1), (9, 4), (4, 5), (3, 8), (1, 7), (9, 6), (3, 3),
+    (9, 1), (9, 7), (3, 4), (1, 0), (4, 2), (5, 5), (4, 8), (3, 7), (3, 6), (9, 0),
+    (4, 9), (4, 4), (6, 5), (5, 8), (6, 8), (6, 9), (3, 1), (6, 2), (3, 0), (4, 7),
+    (6, 4), (5, 2), (7, 5), (4, 6), (4, 3), (5, 9), (7, 9), (4, 1), (7, 2), (4, 0),
+    (6, 7), (6, 6), (6, 3), (6, 1), (7, 4), (5, 3), (5, 6), (7, 8), (6, 0), (5, 4),
+    (8, 9), (7, 6), (7, 7), (8, 2), (5, 7), (7, 1), (5, 1), (5, 0), (7, 3), (8, 5),
+    (7, 0), (8, 8), (8, 6), (8, 4), (8, 7), (8, 1), (8, 3), (8, 0),
 )
 LAST_ORDER = (
-    (0, 5), (0, 6), (0, 9), (0, 0), (1, 5), (0, 3), (1, 9), (1, 6), (0, 2), (1, 0),
-    (9, 5), (2, 5), (9, 6), (1, 3), (2, 6), (9, 3), (0, 1), (2, 9), (1, 2), (9, 0),
-    (2, 0), (3, 5), (0, 4), (2, 3), (0, 7), (3, 6), (1, 1), (9, 2), (0, 8), (2, 2),
-    (3, 0), (3, 3), (1, 4), (9, 9), (1, 7), (4, 5), (9, 4), (2, 1), (3, 2), (1, 8),
-    (2, 4), (9, 1), (9, 7), (3, 9), (9, 8), (2, 7), (2, 8), (3, 1), (3, 4), (4, 6),
-    (3, 8), (4, 3), (3, 7), (4, 9), (4, 2), (4, 8), (4, 1), (4, 0), (4, 4), (4, 7),
+    (0, 8), (0, 5), (0, 6), (0, 0), (0, 4), (0, 2), (10, 5), (1, 8), (0, 3), (0, 1),
+    (2, 5), (0, 7), (2, 6), (10, 6), (2, 2), (1, 5), (9, 5), (10, 4), (10, 0), (10, 1),
+    (2, 0), (2, 4), (2, 8), (9, 8), (10, 7), (2, 1), (10, 2), (1, 6), (2, 7), (9, 6),
+    (0, 9), (3, 5), (1, 1), (2, 3), (9, 1), (3, 8), (10, 3), (1, 2), (9, 2), (1, 4),
+    (3, 6), (1, 0), (9, 0), (9, 4), (1, 7), (3, 1), (1, 3), (1, 9), (3, 2), (9, 7),
+    (3, 4), (9, 3), (2, 9), (3, 0), (4, 1), (4, 6), (3, 3), (9, 9), (3, 7), (4, 2),
+    (3, 9), (4, 8), (4, 4), (4, 3), (4, 7), (4, 5), (4, 0), (4, 9),
 )
+ALONG_Z = ((0, 1, 2, 3, 4, 5, 6, 7), (0, 1, 2, 3, 4, 5, 6, 7))
 
 
 def rope_tables(tokens):
@@ -160,7 +163,7 @@
         rs_sent = [send_group() for _ in range(2)]
         shift_sent = [send_group() for _ in range(2)]
         ag_sem = {(c, k): arrival() for c in range(C) for k in ("z", "y", "far", "rest")}
-        rs_sem = {(c, k): arrival() for c in range(C) for k in ("far", "z", "own")}
+        rs_sem = {(c, k): arrival() for c in range(C) for k in ("q", "a", "z", "own")}
 
         ag = {}
         for l in range(2):
@@ -252,47 +255,51 @@
                     else:
                         ACC[g, j] = ACC[g, j] + part
 
-        def attend(l):
-            power = jnp.sum(SS[...], axis=-1, keepdims=True) * (1.0 / width)
-            factor = lax.rsqrt(power + EPS)
-            heads = [(g, i) for g in range(2) for i in range(heads_each)]
-
-            def rotated(v):
-                return v * TAB[0] + pltpu.roll(v, HD // 2, 1) * TAB[1]
-
-            for h, (g, i) in enumerate(heads):
-                KV[l, 1, h] = (ACC[g, 2, :, i * HD:(i + 1) * HD] * factor).astype(jnp.bfloat16)
-            values = message(KV.at[l, 1], KVO.at[l, 1], partner, send_group(), arrival())
-            keys = message(KV.at[l, 0], KVO.at[l, 0], partner, send_group(), arrival())
-
-            @pl.when(core == 0)
-            def _():
-                values.start()
-
-            for h, (g, i) in enumerate(heads):
-                KV[l, 0, h] = rotated(ACC[g, 1, :, i * HD:(i + 1) * HD] * factor).astype(jnp.bfloat16)
-
-            @pl.when(core == 0)
-            def _():
-                keys.start()
-
-            unsent_early.append(values)
-            unsent_early.append(keys)
+        def prepare(l):
             mine = jnp.broadcast_to(SEGS[l, core, 0:1], (HD, half)).astype(jnp.float32).T[:, 0:1]
             row_of = lax.broadcasted_iota(jnp.int32, (half, half), 0)
             column_of = lax.broadcasted_iota(jnp.int32, (half, half), 1)
             same = mine == SEGS[l, core, 0:1].astype(jnp.float32)
             BIAS[0] = jnp.where(same & (column_of <= row_of), 0.0, MASKED)
-
-            @pl.when(core == 1)
-            def _():
-                BIAS[1] = jnp.where(mine == SEGS[l, 0, 0:1].astype(jnp.float32), 0.0, MASKED)
-
+            BIAS[1] = jnp.where(mine == SEGS[l, 0, 0:1].astype(jnp.float32), 0.0, MASKED)
+
+        def attend(l):
+            power = jnp.sum(SS[...], axis=-1, keepdims=True) * (1.0 / width)
+            factor = lax.rsqrt(power + EPS)
+            heads = [(g, i) for g in range(2) for i in range(heads_each)]
+
+            def rotated(v):
+                return v * TAB[0] + pltpu.roll(v, HD // 2, 1) * TAB[1]
+
+            for h, (g, i) in enumerate(heads):
+                KV[l, 1, h] = (ACC[g, 2, :, i * HD:(i + 1) * HD] * factor).astype(jnp.bfloat16)
+            values = message(KV.at[l, 1], KVO.at[l, 1], partner, send_group(), arrival())
+            keys = message(KV.at[l, 0], KVO.at[l, 0], partner, send_group(), arrival())
+
+            @pl.when(core == 0)
+            def _():
+                values.start()
+
+            for h, (g, i) in enumerate(heads):
+                KV[l, 0, h] = rotated(ACC[g, 1, :, i * HD:(i + 1) * HD] * factor).astype(jnp.bfloat16)
+
+            @pl.when(core == 0)
+            def _():
+                keys.start()
+
+            unsent_early.append(values)
+            unsent_early.append(keys)
             for h, (g, i) in enumerate(heads):
                 q = rotated(ACC[g, 0, :, i * HD:(i + 1) * HD] * factor).astype(jnp.bfloat16)
                 MX[:, h * HD:(h + 1) * HD] = q
                 scores = lax.dot_general(q, KV[l, 0, h], (((1,), (1,)), ((), ())), preferred_element_type=jnp.float32)
-                S[h] = scores * HD ** (-0.5) + BIAS[0]
+                near = scores * HD ** (-0.5) + BIAS[0]
+                top = jnp.max(near, axis=-1, keepdims=True)
+                near = jnp.exp(near - top)
+                total = jnp.sum(near, axis=-1, keepdims=True)
+                S[h, :, 0:HD] = jnp.broadcast_to(top, (half, HD))
+                S[h, :, HD:2 * HD] = jnp.broadcast_to(total, (half, HD))
+                S[h, :, 2 * HD:] = jnp.dot(near.astype(jnp.bfloat16), KV[l, 1, h], preferred_element_type=jnp.float32)
 
             def columns(h):
                 return slice(h * HD, (h + 1) * HD)
@@ -300,11 +307,7 @@
             @pl.when(core == 0)
             def _():
                 for h in range(len(heads)):
-                    near = S[h]
-                    near = jnp.exp(near - jnp.max(near, axis=-1, keepdims=True))
-                    total = jnp.sum(near, axis=-1, keepdims=True)
-                    mixed = jnp.dot(near.astype(jnp.bfloat16), KV[l, 1, h], preferred_element_type=jnp.float32)
-                    MX[:, columns(h)] = (mixed / total).astype(jnp.bfloat16)
+                    MX[:, columns(h)] = (S[h, :, 2 * HD:] / S[h, :, HD:2 * HD]).astype(jnp.bfloat16)
 
             @pl.when(core == 1)
             def _():
@@ -312,17 +315,16 @@
                     values.wait_recv()
                     keys.wait_recv()
                 for h in range(len(heads)):
-                    q = MX[:, columns(h)]
-                    near = S[h]
                     away = lax.dot_general(
-                        q, KVO[l, 0, h], (((1,), (1,)), ((), ())), preferred_element_type=jnp.float32
+                        MX[:, columns(h)], KVO[l, 0, h], (((1,), (1,)), ((), ())), preferred_element_type=jnp.float32
                     )
                     away = away * HD ** (-0.5) + BIAS[1]
-                    top = jnp.maximum(jnp.max(near, axis=-1, keepdims=True), jnp.max(away, axis=-1, keepdims=True))
-                    near = jnp.exp(near - top)
-                    away = jnp.exp(away - top)
-                    total = jnp.sum(near, axis=-1, keepdims=True) + jnp.sum(away, axis=-1, keepdims=True)
-                    mixed = jnp.dot(near.astype(jnp.bfloat16), KV[l, 1, h], preferred_element_type=jnp.float32)
+                    before = S[h, :, 0:HD]
+                    top = jnp.maximum(before, jnp.max(away, axis=-1, keepdims=True))
+                    kept = jnp.exp(before - top)
+                    away = jnp.exp(away - top[:, 0:1])
+                    total = S[h, :, HD:2 * HD] * kept + jnp.sum(away, axis=-1, keepdims=True)
+                    mixed = S[h, :, 2 * HD:] * kept
                     mixed = mixed + jnp.dot(away.astype(jnp.bfloat16), KVO[l, 1, h], preferred_element_type=jnp.float32)
                     MX[:, columns(h)] = (mixed / total).astype(jnp.bfloat16)
 
@@ -333,14 +335,18 @@
                     return message(PB.at[l, c, rows(b)], R.at[l, c, slot], device, rs_sent[l], rs_sem[c, kind])
                 even = c % 2 == 0
                 rs[l, c] = dict(
-                    a0=part(far if even else z_far, 0, dev_up, "far"),
-                    a1=part(z_far if even else far, 1, dev_down, "far"),
                     b2=part(z_up, 2, dev_up, "z"),
                     b3=part(z_down, 3, dev_down, "z"),
                     b0=part(up, 4, dev_up, "own"),
                     b1=part(down, 5, dev_down, "own"),
                     z=part(rz, 6, dev_z, "own"),
                 )
+                if c in ALONG_Z[l]:
+                    rs[l, c].update(q=part(z_far, 0, dev_z, "q"), a=part(far, 1, dev_up if even else dev_down, "a"))
+                else:
+                    rs[l, c].update(
+                        a0=part(far if even else z_far, 0, dev_up, "q"), a1=part(z_far if even else far, 1, dev_down, "a")
+                    )
         shift_sem = [[arrival() for _ in range(C)] for _ in range(2)]
         shifts = {}
         for c in range(C):
@@ -355,17 +361,26 @@
                 MX[...], O[:, :, c * cw:(c + 1) * cw].reshape(2 * cols, cw), preferred_element_type=jnp.float32
             ).astype(jnp.bfloat16)
             m = rs[l, c]
-            for name in ("a0", "a1", "b2") if c % 2 == 0 else ("a0", "a1", "b3"):
+            for name in ("q", "b2", "b3") if c in ALONG_Z[l] else ("a0", "a1", "b2" if c % 2 == 0 else "b3"):
                 m[name].start()
 
+        def fold(l, c, slot, kind, b):
+            wait_for(R.at[l, c, slot], rs_sem[c, kind])
+            r = rows(b)
+            PB[l, c, r] = (f32(PB[l, c, r]) + f32(R[l, c, slot])).astype(jnp.bfloat16)
+
         def fold_far(l, c):
-            m = rs[l, c]
-            wait_for(R.at[l, c, pl.ds(0, 2)], rs_sem[c, "far"])
+            fold(l, c, 0, "q", far)
+            rs[l, c]["a"].start()
+
+        def fold_y(l, c):
             even = c % 2 == 0
-            for slot, b in ((0, up if even else z_up), (1, z_down if even else down)):
-                r = rows(b)
-                PB[l, c, r] = (f32(PB[l, c, r]) + f32(R[l, c, slot])).astype(jnp.bfloat16)
-            m["b3" if even else "b2"].start()
+            if c in ALONG_Z[l]:
+                fold(l, c, 1, "a", up if even else down)
+                return
+            fold(l, c, 0, "q", up if even else z_up)
+            fold(l, c, 1, "a", z_down if even else down)
+            rs[l, c]["b3" if even else "b2"].start()
 
         def give(l, c):
             for name in ("b0", "b1"):
@@ -425,6 +440,13 @@
                 gain_other.wait_recv()
                 gain_waited.append(True)
                 w_own.wait()
+                segments_other.wait_recv()
+
+                @pl.when(jnp.logical_not(last))
+                def _():
+                    segments_ahead.start()
+
+                prepare(0)
             w_other[c].wait_recv()
             multiply(0, c)
 
@@ -435,25 +457,33 @@
             7: lambda c: relay_far(0, c),
             8: compute_first,
         }, FIRST_ORDER)
-        segments_other.wait_recv()
-
-        @pl.when(jnp.logical_not(last))
-        def _():
-            segments_ahead.start()
-
         table_copy.wait()
         with jax.named_scope("attend_first"):
             attend(0)
         o_own.wait()
         o_other.wait_recv()
 
+        def segments_second():
+            @pl.when(first)
+            def _():
+                for b in range(2):
+                    SEGS[1, b] = jnp.broadcast_to(FIN[b:b + 1], (8, half))
+
+            @pl.when(jnp.logical_not(first))
+            def _():
+                segments_ahead.wait_recv()
+            prepare(1)
+
         def compute_second(c):
+            if 1 not in begun:
+                segments_second()
             gathered(1, c)
             multiply(1, c)
 
         run({
             0: lambda c: project(0, c),
-            1: lambda c: fold_far(0, c),
+            1: lambda c: fold_y(0, c),
+            10: lambda c: fold_far(0, c),
             2: lambda c: fold_z(0, c),
             3: lambda c: finish(0, c),
             4: enter,
@@ -464,20 +494,12 @@
             9: lambda c: give(0, c),
         }, MIDDLE_ORDER)
 
-        @pl.when(first)
-        def _():
-            for b in range(2):
-                SEGS[1, b] = jnp.broadcast_to(FIN[b:b + 1], (8, half))
-
-        @pl.when(jnp.logical_not(first))
-        def _():
-            segments_ahead.wait_recv()
-
         with jax.named_scope("attend_second"):
             attend(1)
         run({
             0: lambda c: project(1, c),
-            1: lambda c: fold_far(1, c),
+            1: lambda c: fold_y(1, c),
+            10: lambda c: fold_far(1, c),
             2: lambda c: fold_z(1, c),
             3: lambda c: finish(1, c),
             4: leave,
@@ -523,7 +545,7 @@
         pltpu.VMEM((2, 2, heads, half, HD), bf),
         pltpu.VMEM((2, 2, heads, half, HD), bf),
         pltpu.VMEM((half, heads * HD), bf),
-        pltpu.VMEM((heads, half, half), f4),
+        pltpu.VMEM((heads, half, 3 * HD), f4),
         pltpu.VMEM((2, half, half), f4),
         pltpu.VMEM((2, 8, gw), f4),
         pltpu.VMEM((2, 2, 8, half), jnp.int32),
@@ -533,7 +555,7 @@
         pltpu.VMEM((2, half), jnp.int32),
         pltpu.SemaphoreType.DMA((C + 7,)),
         pltpu.SemaphoreType.DMA((6 + 1 + 4 + 4,)),
-        pltpu.SemaphoreType.DMA(((4 + 3 + 2 + 1) * C + 4 + 4,)),
+        pltpu.SemaphoreType.DMA(((4 + 4 + 2 + 1) * C + 4 + 4,)),
         pltpu.SemaphoreType.DMA((3,)),
     ]
     return kernel, scratch

time: 120 us -> 116 us (0.967)
  the two profiles are of different devices: /device:TPU:1 before, /device:TPU:65 now
where the time goes in v4:
time: 116 us
  Pallas kernels  115 us (99%)
    pallas_call x1, Pallas kernels, per_device(): pl.pallas_call(kernel, name='relay', out_shape=(jax.ShapeDtypeStruct((2,...  113 us

profile of v4, /device:TPU:65, one launch (start us, length us, event | category | flops | bytes accessed | tf_op | source)
XLA Modules:
  0.0 115.8 jit_solution(3585871317440199894)
XLA Ops:
  0.6 112.9 %relay.1 = (bf16[2,1,32,5120]{3,2,1,0:T(8,128)(2,1)}, bf16[1,32,5120]{2,1,0:T(8,128)(2,1)}) custom-call(bf16[1,32,5120]{2,1,0:T(8,128)(2,1)} %carried.1, s32[1,256]{1,0:T(1,128)} %own_segments.1, bf16[2,32,5120]{2,1,0:T(8,128)(2,1)} %fresh.1, s32[2,256]{1,0:T(2,128)} %fresh_segments.1, bf16[3,5120,256]{2,1,0:T(8,128)(2,1)} %bitcast.3, ...), custom_call_target="tpu_custom_call" | custom-call | tf_op jit(solution)/shard_map/relay/pallas_call | solution.py:599
  113.6 2.1 %store.1 = (bf16[2,1,32,5120]{3,2,1,0:T(8,128)(2,1)}, bf16[1,32,5120]{2,1,0:T(8,128)(2,1)}) custom-call(bf16[2,1,32,5120]{3,2,1,0:T(8,128)(2,1)} %get-tuple-element.4.refs_0_, bf16[1,32,5120]{2,1,0:T(8,128)(2,1)} %get-tuple-element.5.refs_1_), custom_call_target="tpu_custom_call" | custom-call | tf_op jit(solution)/shard_map/store/pallas_call | solution.py:580

commit v5 on v4

--- a/solution.py
+++ b/solution.py
@@ -65,7 +65,7 @@
         carried, own_segments, fresh, fresh_segments, w_hbm, o_hbm, gain, tables,
         out, shadow,
         X, W, O, ACC, SS, XG, PB, R, YS, SH, KV, KVO, MX, S, BIAS, G, SEGS, TAB, GIN, SIN, FIN,
-        local_sem, send_sem, recv_sem, out_sem,
+        local_sem, send_sem, recv_sem,
     ):
         p = lax.axis_index("section")
         t = lax.axis_index("tp")
@@ -271,21 +271,21 @@
             def rotated(v):
                 return v * TAB[0] + pltpu.roll(v, HD // 2, 1) * TAB[1]
 
+            values = message(KV.at[l, 1], KVO.at[l, 1], partner, send_group(), arrival())
+            keys = message(KV.at[l, 0], KVO.at[l, 0], partner, send_group(), arrival())
+            for h, (g, i) in enumerate(heads):
+                KV[l, 0, h] = rotated(ACC[g, 1, :, i * HD:(i + 1) * HD] * factor).astype(jnp.bfloat16)
+
+            @pl.when(core == 0)
+            def _():
+                keys.start()
+
             for h, (g, i) in enumerate(heads):
                 KV[l, 1, h] = (ACC[g, 2, :, i * HD:(i + 1) * HD] * factor).astype(jnp.bfloat16)
-            values = message(KV.at[l, 1], KVO.at[l, 1], partner, send_group(), arrival())
-            keys = message(KV.at[l, 0], KVO.at[l, 0], partner, send_group(), arrival())
 
             @pl.when(core == 0)
             def _():
                 values.start()
-
-            for h, (g, i) in enumerate(heads):
-                KV[l, 0, h] = rotated(ACC[g, 1, :, i * HD:(i + 1) * HD] * factor).astype(jnp.bfloat16)
-
-            @pl.when(core == 0)
-            def _():
-                keys.start()
 
             unsent_early.append(values)
             unsent_early.append(keys)
@@ -312,7 +312,6 @@
             @pl.when(core == 1)
             def _():
                 with jax.named_scope("keys_wait"):
-                    values.wait_recv()
                     keys.wait_recv()
                 for h in range(len(heads)):
                     away = lax.dot_general(
@@ -323,6 +322,8 @@
                     top = jnp.maximum(before, jnp.max(away, axis=-1, keepdims=True))
                     kept = jnp.exp(before - top)
                     away = jnp.exp(away - top[:, 0:1])
+                    if h == 0:
+                        values.wait_recv()
                     total = S[h, :, HD:2 * HD] * kept + jnp.sum(away, axis=-1, keepdims=True)
                     mixed = S[h, :, 2 * HD:] * kept
                     mixed = mixed + jnp.dot(away.astype(jnp.bfloat16), KVO[l, 1, h], preferred_element_type=jnp.float32)
@@ -399,7 +400,7 @@
             total = f32(PB[l, c, r]) + f32(R[l, c, 4]) + f32(R[l, c, 5]) + f32(R[l, c, 6])
             result = (f32(X[l, c, r]) + total).astype(jnp.bfloat16)
             YS[l, c] = result
-            pltpu.make_async_copy(YS.at[l, c], out.at[l, 0, :, span(c)], out_sem.at[l]).start()
+            out[l, 0, :, c * cw:(c + 1) * cw] = result
 
             @pl.when(jnp.logical_not(last) if l == 0 else jnp.logical_not(first))
             def _():
@@ -425,7 +426,7 @@
             def _():
                 shifts[1, c].wait_recv()
 
-            pltpu.make_async_copy(SH.at[c], shadow.at[0, :, span(c)], out_sem.at[2]).start()
+            shadow[0, :, c * cw:(c + 1) * cw] = SH[c]
 
         def run(steps, order):
             for k, c in order:
@@ -510,8 +511,6 @@
                 wait_for(R.at[l], ag_sent[l])
                 wait_for(R.at[l], rs_sent[l])
             wait_for(W.at[core], w_sent)
-            for ref, n in ((YS.at[0], 0), (YS.at[1], 1), (SH, 2)):
-                wait_for(ref, out_sem.at[n])
             for copy in (gain_other, segments_other, o_other):
                 copy.wait_send()
 
@@ -556,35 +555,32 @@
         pltpu.SemaphoreType.DMA((C + 7,)),
         pltpu.SemaphoreType.DMA((6 + 1 + 4 + 4,)),
         pltpu.SemaphoreType.DMA(((4 + 4 + 2 + 1) * C + 4 + 4,)),
-        pltpu.SemaphoreType.DMA((3,)),
     ]
     return kernel, scratch
 
 
 def store(count):
     def kernel(*refs):
-        sources, results, held, sem = refs[:count], refs[count:2 * count], refs[2 * count:3 * count], refs[-1]
+        sources, results, sem = refs[:count], refs[count:2 * count], refs[-1]
         for i in range(count):
-            pltpu.make_async_copy(sources[i], held[i], sem.at[0, i]).start()
+            pltpu.make_async_copy(sources[i], results[i], sem.at[i]).start()
         for i in range(count):
-            pltpu.make_async_copy(sources[i], held[i], sem.at[0, i]).wait()
-            pltpu.make_async_copy(held[i], results[i], sem.at[1, i]).start()
-        for i in range(count):
-            pltpu.make_async_copy(held[i], results[i], sem.at[1, i]).wait()
+            pltpu.make_async_copy(sources[i], results[i], sem.at[i]).wait()
 
     return kernel
 
 
 def carry_over(arrays):
     hbm = pl.BlockSpec(memory_space=pl.ANY)
+    vmem = pl.BlockSpec(memory_space=pltpu.VMEM)
     return pl.pallas_call(
         store(len(arrays)),
         name="store",
         out_shape=tuple(jax.ShapeDtypeStruct(a.shape, a.dtype) for a in arrays),
-        in_specs=[hbm] * len(arrays),
+        in_specs=[vmem] * len(arrays),
         out_specs=(hbm,) * len(arrays),
-        scratch_shapes=[pltpu.VMEM(a.shape, a.dtype) for a in arrays] + [pltpu.SemaphoreType.DMA((2, len(arrays)))],
-        compiler_params=pltpu.CompilerParams(vmem_limit_bytes=60 * 2**20),
+        scratch_shapes=[pltpu.SemaphoreType.DMA((len(arrays),))],
+        compiler_params=pltpu.CompilerParams(vmem_limit_bytes=2**20),
     )(*arrays)
 
 
@@ -596,15 +592,16 @@
     weights = jnp.transpose(qkv_weight[0], (1, 0, 2))
     tables = jnp.asarray(rope_tables(16 * block))
     hbm = pl.BlockSpec(memory_space=pltpu.HBM)
+    vmem = pl.BlockSpec(memory_space=pltpu.VMEM)
     out, shadow = pl.pallas_call(
         kernel,
         name="relay",
         out_shape=(
-            jax.ShapeDtypeStruct((2, 1, block, width), jnp.bfloat16),
-            jax.ShapeDtypeStruct((1, block, width), jnp.bfloat16),
+            pltpu.VMEM((2, 1, block, width), jnp.bfloat16),
+            pltpu.VMEM((1, block, width), jnp.bfloat16),
         ),
         in_specs=[hbm] * 8,
-        out_specs=(hbm, hbm),
+        out_specs=(vmem, vmem),
         scratch_shapes=scratch,
         compiler_params=pltpu.CompilerParams(
             collective_id=0, has_side_effects=True, vmem_limit_bytes=60 * 2**20

time: 116 us -> 114 us (0.983)
  the two profiles are of different devices: /device:TPU:65 before, /device:TPU:1 now
where the time goes in v5:
time: 114 us; the launch traced here: 112 us
  Pallas kernels  111 us (97%)
    pallas_call x1, Pallas kernels, per_device(): pl.pallas_call(kernel, name='relay', out_shape=(pltpu.VMEM((2, 1, block,...  110 us

profile of v5, /device:TPU:1, one launch (start us, length us, event | category | flops | bytes accessed | tf_op | source)
XLA Modules:
  0.0 112.1 jit_solution(3044287278341870213)
XLA Ops:
  0.6 110.4 %relay.1 = (bf16[2,1,32,5120]{3,2,1,0:T(8,128)(2,1)S(1)}, bf16[1,32,5120]{2,1,0:T(8,128)(2,1)S(1)}) custom-call(bf16[1,32,5120]{2,1,0:T(8,128)(2,1)} %carried.1, s32[1,256]{1,0:T(1,128)} %own_segments.1, bf16[2,32,5120]{2,1,0:T(8,128)(2,1)} %fresh.1, s32[2,256]{1,0:T(2,128)} %fresh_segments.1, bf16[3,5120,256]{2,1,0:T(8,128)(2,1)} %bitcast.3, ...), custom_call_target="tpu_custom_call" | custom-call | tf_op jit(solution)/shard_map/relay/pallas_call | solution.py:596
  111.0 1.0 store.1
